TPU v7x, 32 devices: a whole 2x2x4 slice. The times are simulated.
32 devices in a mesh: seq: 8 (over z, core), vocab: 4 (over y, x).
Axes of the slice: x: 2, y: 2, z: 4, core: 2. Of those that a mesh axis runs over, the one named last changes fastest.
Arguments:
- probe_states: bfloat16 [3, 8192, 6144], P(None, 'seq', 'vocab'), may hold values from -6 to 6
- final_states: bfloat16 [8192, 6144], P('seq', 'vocab'), may hold values from -6 to 6
- translator: bfloat16 [3, 6144, 6144], P(None, 'vocab', 'seq'), may hold values from -0.078125 to 0.078125
- translator_bias: float32 [3, 6144], P(None, 'seq'), may hold values from -4 to 4
- norm_gain: float32 [6144], P('seq'), may hold values from 0.5 to 1.5
- unembed: bfloat16 [32768, 6144], P('vocab', 'seq'), may hold values from -0.21875 to 0.21875
- answer_rows: int32 [8, 32], P('seq'), may hold values from 0 to 1023, as said below
- answer_count: int32 [8], P('seq'), may hold values from 1 to 32, 128 in all
- targets: int32 [8, 32], P('seq'), may hold values from 0 to 32767
Outputs:
- answer_logprob: float32 [4, 8, 32], P(None, 'seq')
- answer_kl: float32 [3, 8, 32], P(None, 'seq')
Inputs may be any that keep to these rules, and one draw needn't show every extreme that they name: `answer_rows`: each row holds 32 different positions. `answer_count`: the counts sum to 128, and some sequence has 32.
All inputs are finite; a program needn't handle non-finite values. No bound on the sum of `answer_count` on one device may be relied on, other than what follows from the above.
Results may differ from a plain program's by a relative error of at most 0.00099.
Values may be sent and summed in bfloat16 or wider, within the bound.
A program may use at most 128 MiB of HBM per device.

v0:
```python
import math
import jax
import jax.numpy as jnp
from jax import lax
from jax.experimental import pallas as pl
from jax.experimental.pallas import tpu as pltpu
from jax.sharding import PartitionSpec as P

FLAG_DEV = 16
STATE_MAX, MATRIX_MAX, BIAS_MAX, GAIN_MAX, UNEMBED_MAX = 6.0, 0.078125, 4.0, 1.5, 0.21875
CHUNKS = 4
LAG = 2
SLOTS = 4
MESH = pl.DeviceIdType.MESH
f32, bf16, i16, i32 = jnp.float32, jnp.bfloat16, jnp.int16, jnp.int32


class Code:
    def __init__(self, model):
        widest = GAIN_MAX * UNEMBED_MAX * model * (STATE_MAX + BIAS_MAX + model * STATE_MAX * MATRIX_MAX)
        self.knee = 7.5e-4
        self.scale = 32700.0 / math.log2(1.0 + 1.02 * widest / self.knee)

    def enc(self, value):
        level = jnp.log2(1.0 + jnp.abs(value) * (1.0 / self.knee)) * self.scale
        return jnp.round(jnp.where(value < 0, -level, level)).astype(i32).astype(i16)

    def dec(self, code):
        level = code.astype(i32).astype(f32)
        size = (jnp.exp2(jnp.abs(level) * (1.0 / self.scale)) - 1.0) * self.knee
        return jnp.where(level < 0, -size, size)


def kernel(
    layers, total, seq_count, vocab_count, code,
    y_ref, fac_ref, tgt_ref, u_hbm, out_ref,
    u, own, psend, precv, zsend, zrecv, z3, e3, acc, stat_send, stat_recv, line_send, line_recv,
    u_sem, psend_sem, precv_sem, zsend_sem, zrecv_sem, ssend_sem, srecv_sem, lsend_sem, lrecv_sem,
):
    seq, voc = lax.axis_index("seq"), lax.axis_index("vocab")
    chip, core = seq // 2, seq % 2
    chips = seq_count // 2
    vp, _ = u.shape
    half, quarter = vp // 2, vp // 4
    chunk = quarter // CHUNKS
    steps = layers * CHUNKS
    plane = 2 * vocab_count
    me = core * vocab_count + voc
    at_end = jnp.logical_or(chip == 0, chip == chips - 1)

    pieces = 4 * CHUNKS
    piece = vp // pieces

    def u_copy(k):
        rows = pl.ds(pl.multiple_of(k * piece, piece), piece)
        return pltpu.make_async_copy(u_hbm.at[rows], u.at[rows], u_sem.at[k])

    @pl.loop(0, pieces)
    def _(k):
        u_copy(k).start()

    barrier = pltpu.get_barrier_semaphore()

    def in_plane(p):
        q = lax.rem(me + p, plane)
        return q, (chip * 2 + q // vocab_count, lax.rem(q, vocab_count))

    def in_line(p):
        q = lax.rem(chip + p, chips)
        return q, (q * 2 + core, voc)

    @pl.loop(1, plane)
    def _(p):
        pl.semaphore_signal(barrier, inc=1, device_id=in_plane(p)[1], device_id_type=MESH)

    @pl.loop(1, chips)
    def _(p):
        pl.semaphore_signal(barrier, inc=1, device_id=in_line(p)[1], device_id_type=MESH)

    pl.semaphore_wait(barrier, plane - 1 + chips - 1)
    acc[...] = jnp.zeros_like(acc)

    def pair_copy(t):
        return pltpu.make_async_remote_copy(
            src_ref=psend.at[lax.rem(t, SLOTS)], dst_ref=precv.at[t],
            send_sem=psend_sem.at[lax.rem(t, SLOTS)], recv_sem=precv_sem.at[t],
            device_id=(chip * 2 + 1 - core, voc), device_id_type=MESH,
        )

    def line_copy(k, d):
        to = jnp.minimum(chip + 1, chips - 1) if d == 0 else jnp.maximum(chip - 1, 0)
        return pltpu.make_async_remote_copy(
            src_ref=zsend.at[k, d], dst_ref=zrecv.at[k, d],
            send_sem=zsend_sem.at[k, d], recv_sem=zrecv_sem.at[k, d],
            device_id=(to * 2 + core, voc), device_id_type=MESH,
        )

    def rows_at(owner, d, j):
        start = owner * half + d * quarter + j * chunk
        return pl.ds(pl.multiple_of(start, chunk), chunk)

    def product(rows, yl):
        return lax.dot_general(u[rows, :], yl, (((1,), (1,)), ((), ())), preferred_element_type=f32)

    def fold(value):
        return jnp.sum(value.reshape(chunk // 8, 8, total), axis=0)

    def finish(k, d, value):
        rank, j = k // CHUNKS, lax.rem(k, CHUNKS)
        layer = lax.rem(rank + layers - 1, layers)
        logit = value * fac_ref[layer]
        base = voc * vp + core * half + d * quarter + j * chunk
        spot = lax.broadcasted_iota(i32, (chunk, total), 0) + base
        grown = jnp.exp(logit)
        acc[layer] += fold(grown)
        acc[layers + layer] += fold(jnp.where(spot == tgt_ref[...], logit, 0.0))

        @pl.when(rank == 0)
        def _():
            z3[j] = logit
            e3[j] = grown

        @pl.when(rank > 0)
        def _():
            acc[2 * layers + layer] += fold(e3[j] * (z3[j] - logit))

    def forward(k, d):
        first = chip == (0 if d == 0 else chips - 1)
        last = chip == (chips - 1 if d == 0 else 0)

        @pl.when(jnp.logical_not(first))
        def _():
            line_copy(k, d).wait_recv()
            own[k, d] = own[k, d] + code.dec(zrecv[k, d])

        @pl.when(jnp.logical_not(last))
        def _():
            zsend[k, d] = code.enc(own[k, d])
            line_copy(k, d).start()

        @pl.when(last)
        def _():
            finish(k, d, own[k, d])

    @pl.loop(0, steps + 1 + LAG * (chips - 1))
    def _(t):
        @pl.when(t < CHUNKS)
        def _():
            for part in range(4):
                u_copy(part * CHUNKS + t).wait()

        @pl.when(t < steps)
        def _():
            layer, j = lax.rem(t // CHUNKS + layers - 1, layers), lax.rem(t, CHUNKS)
            yl = y_ref[pl.ds(pl.multiple_of(layer * total, total), total), :]

            @pl.when(t >= SLOTS)
            def _():
                pair_copy(t - SLOTS).wait_send()

            for d in range(2):
                psend[lax.rem(t, SLOTS), d] = product(rows_at(1 - core, d, j), yl)
            pair_copy(t).start()
            for d in range(2):
                own[t, d] = product(rows_at(core, d, j), yl)

        @pl.when(jnp.logical_and(t >= 1, t <= steps))
        def _():
            pair_copy(t - 1).wait_recv()
            own[t - 1] = own[t - 1] + precv[t - 1]

        for d in range(2):
            k = t - 1 - LAG * (chip if d == 0 else chips - 1 - chip)

            @pl.when(jnp.logical_and(k >= 0, k < steps))
            def _():
                forward(k, d)

    @pl.loop(steps - SLOTS, steps)
    def _(t):
        pair_copy(t).wait_send()

    @pl.loop(0, steps)
    def _(k):
        for d in range(2):
            @pl.when(chip != (chips - 1 if d == 0 else 0))
            def _():
                line_copy(k, d).wait_send()

    def stat_copy(p):
        _, there = in_plane(p)
        return pltpu.make_async_remote_copy(
            src_ref=stat_send, dst_ref=stat_recv.at[me], send_sem=ssend_sem.at[p], recv_sem=srecv_sem.at[me],
            device_id=there, device_id_type=MESH,
        )

    def stat_arrival(p):
        q, there = in_plane(p)
        return pltpu.make_async_remote_copy(
            src_ref=stat_send, dst_ref=stat_recv.at[q], send_sem=ssend_sem.at[p], recv_sem=srecv_sem.at[q],
            device_id=there, device_id_type=MESH,
        )

    end = jnp.where(chip == 0, 0, 1)

    def line_stat(p):
        _, there = in_line(p)
        return pltpu.make_async_remote_copy(
            src_ref=line_send, dst_ref=line_recv.at[end], send_sem=lsend_sem.at[p], recv_sem=lrecv_sem.at[end],
            device_id=there, device_id_type=MESH,
        )

    def line_arrival(side):
        return pltpu.make_async_remote_copy(
            src_ref=line_send, dst_ref=line_recv.at[side], send_sem=lsend_sem.at[0], recv_sem=lrecv_sem.at[side],
            device_id=in_line(1)[1], device_id_type=MESH,
        )

    @pl.when(at_end)
    def _():
        stat = jnp.concatenate(
            [jnp.sum(acc[i], axis=0, keepdims=True) for i in range(3 * layers)]
            + [jnp.zeros((stat_send.shape[0] - 3 * layers, total), f32)], axis=0,
        )
        stat_send[...] = stat
        stat_recv[me] = stat

        @pl.loop(1, plane)
        def _(p):
            stat_copy(p).start()

        @pl.loop(1, plane)
        def _(p):
            stat_arrival(p).wait_recv()

        full = stat_recv[0]
        for q in range(1, plane):
            full = full + stat_recv[q]
        line_send[...] = full
        line_recv[end] = full

        @pl.loop(1, chips)
        def _(p):
            line_stat(p).start()

        @pl.loop(1, plane)
        def _(p):
            stat_copy(p).wait_send()

    for side in range(2):
        @pl.when(chip != (0 if side == 0 else chips - 1))
        def _():
            line_arrival(side).wait_recv()

    @pl.when(at_end)
    def _():
        @pl.loop(1, chips)
        def _(p):
            line_stat(p).wait_send()

    full = line_recv[0] + line_recv[1]
    total_exp, picked = full[:layers], full[layers : 2 * layers]
    cross = full[2 * layers : 3 * layers - 1]
    log_total = jnp.log(total_exp)
    gone = cross / total_exp[layers - 1 :] - log_total[layers - 1 :] + log_total[: layers - 1]
    spare = jnp.zeros((out_ref.shape[0] - 2 * layers + 1, total), f32)
    out_ref[...] = jnp.concatenate([picked - log_total, gone, spare], axis=0)


def readout(y, fac, tgt, unembed, layers, total, seq_count, vocab_count, model):
    vp, width = unembed.shape
    steps = layers * CHUNKS
    chunk = vp // 4 // CHUNKS
    plane = 2 * vocab_count
    code = Code(model)
    deep = -(-3 * layers // 8) * 8
    dma = pltpu.SemaphoreType.DMA
    vmem = pl.BlockSpec(memory_space=pltpu.VMEM)
    body = lambda *refs: kernel(layers, total, seq_count, vocab_count, code, *refs)
    return pl.pallas_call(
        body,
        out_shape=jax.ShapeDtypeStruct((deep, total), f32),
        in_specs=[vmem, vmem, vmem, pl.BlockSpec(memory_space=pl.ANY)],
        out_specs=vmem,
        scratch_shapes=[
            pltpu.VMEM((vp, width), bf16),
            pltpu.VMEM((steps, 2, chunk, total), f32),
            pltpu.VMEM((SLOTS, 2, chunk, total), f32),
            pltpu.VMEM((steps, 2, chunk, total), f32),
            pltpu.VMEM((steps, 2, chunk, total), i16),
            pltpu.VMEM((steps, 2, chunk, total), i16),
            pltpu.VMEM((CHUNKS, chunk, total), f32),
            pltpu.VMEM((CHUNKS, chunk, total), f32),
            pltpu.VMEM((3 * layers, 8, total), f32),
            pltpu.VMEM((deep, total), f32),
            pltpu.VMEM((plane, deep, total), f32),
            pltpu.VMEM((deep, total), f32),
            pltpu.VMEM((2, deep, total), f32),
            dma((4 * CHUNKS,)),
            dma((SLOTS,)),
            dma((steps,)),
            dma((steps, 2)),
            dma((steps, 2)),
            dma((plane,)),
            dma((plane,)),
            dma((seq_count // 2,)),
            dma((2,)),
        ],
        compiler_params=pltpu.CompilerParams(
            collective_id=0, has_side_effects=True, vmem_limit_bytes=62 << 20
        ),
        name="readout",
    )(y, fac, tgt, unembed)


def body(
    probe_states,
    final_states,
    translator,
    translator_bias,
    norm_gain,
    unembed,
    answer_rows,
    answer_count,
    targets,
):
    f32 = jnp.float32
    bf16 = jnp.bfloat16
    seq_count = lax.axis_size("seq")
    vocab_count = lax.axis_size("vocab")
    seq_index = lax.axis_index("seq")
    vocab_index = lax.axis_index("vocab")
    layers = probe_states.shape[0]
    cap = answer_rows.shape[1]
    width_in = probe_states.shape[2]
    width_out = translator.shape[2]
    vocab_part = unembed.shape[0]
    model = width_in * vocab_count
    total = seq_count * FLAG_DEV
    stacked = (layers + 1) * total
    picks = answer_rows[0]

    probed = jnp.take(probe_states, picks, axis=1, mode="clip")
    local = jnp.concatenate(
        [probed[l] for l in range(layers)] + [jnp.take(final_states, picks, axis=0, mode="clip")],
        axis=1,
    )
    gathered = lax.all_gather(local, "seq", axis=0, tiled=True)
    meta = lax.all_gather(
        jnp.concatenate([answer_count[None, :], targets], axis=1), "seq", axis=0, tiled=True
    )
    counts, targets_all = meta[:, 0], meta[:, 1:]
    order = jnp.arange(seq_count, dtype=jnp.int32)
    starts = jnp.sum(jnp.where(order[:, None] < order[None, :], counts[:, None], 0), axis=0)
    slots = jnp.arange(cap, dtype=jnp.int32)
    place = jnp.where(slots[None, :] < counts[:, None], starts[:, None] + slots[None, :], -1)
    hit = place.reshape(-1)[None, :] == jnp.arange(total, dtype=jnp.int32)[:, None]
    row_targets = jnp.sum(jnp.where(hit, targets_all.reshape(-1)[None, :], 0), axis=1)

    rows = jnp.dot(hit.astype(bf16), gathered, preferred_element_type=f32).astype(bf16)
    parts = [rows[:, l * width_in : (l + 1) * width_in] for l in range(layers + 1)]
    in_pos = vocab_index * width_in + jnp.arange(width_in, dtype=jnp.int32)
    out_pos = seq_index * width_out + jnp.arange(width_out, dtype=jnp.int32)
    identity = (in_pos[:, None] == out_pos[None, :]).astype(bf16)
    bias = jnp.where(vocab_index == 0, translator_bias, 0.0)
    pieces = []
    for l in range(layers + 1):
        piece = jnp.dot(parts[l], identity, preferred_element_type=f32)
        if l < layers:
            piece = piece + jnp.dot(parts[l], translator[l], preferred_element_type=f32) + bias[l]
        pieces.append(piece)
    partial_value = jnp.concatenate(pieces, axis=0)
    lensed = lax.psum_scatter(partial_value, "vocab", scatter_dimension=0, tiled=True)
    squares = jnp.sum(lensed * lensed, axis=1)
    scaled = lax.all_gather(
        (lensed * norm_gain[None, :]).astype(bf16), "vocab", axis=0, tiled=True
    )
    chunk = stacked // vocab_count
    spread = jnp.where(
        jnp.arange(vocab_count, dtype=jnp.int32)[:, None] == vocab_index,
        squares.reshape(1, chunk),
        0.0,
    )
    every_square = lax.psum(lax.psum(spread, "vocab"), "seq").reshape(stacked)
    factor = lax.rsqrt(every_square / model + 1e-05)

    results = readout(
        scaled,
        factor.reshape(layers + 1, 1, total),
        row_targets.reshape(1, total),
        unembed,
        layers + 1,
        total,
        seq_count,
        vocab_count,
        model,
    )[: 2 * layers + 1]
    mine = lax.dynamic_slice_in_dim(place, seq_index, 1, axis=0)
    own = mine.reshape(cap, 1) == jnp.arange(total, dtype=jnp.int32)[None, :]
    out = jnp.sum(jnp.where(own[None], results[:, None, :], 0.0), axis=2)
    return (out[: layers + 1, None, :], out[layers + 1 :, None, :])


def solution(mesh):
    in_specs = (
        P(None, "seq", "vocab"),
        P("seq", "vocab"),
        P(None, "vocab", "seq"),
        P(None, "seq"),
        P("seq"),
        P("vocab", "seq"),
        P("seq", None),
        P("seq"),
        P("seq", None),
    )
    out_specs = (P(None, "seq", None), P(None, "seq", None))
    return jax.shard_map(body, mesh=mesh, in_specs=in_specs, out_specs=out_specs, check_vma=False)
```

profile of v0, /device:TPU:0, one launch (start us, length us, event | category | flops | bytes accessed | tf_op | source)
XLA Modules:
  0.0 213.6 jit_solution(4073378094549786422)
XLA Ops:
  7.2 0.7 pad_clamp_fusion
  7.9 2.1 gather_fusion
  10.0 3.0 %gather_fusion.1 = bf16[32,1536]{1,0:T(8,128)(2,1)S(1)} fusion(bf16[1024,1536]{1,0:T(8,128)(2,1)} %param.10, s32[1024]{0:T(1024)S(1)} %pad_clamp_fusion), kind=kCustom, calls=%fused_computation.1 | custom fusion | bytes 196736 | tf_op jit(solution)/shard_map/jit(_take)/gather | solution.py:345
  13.0 0.8 pad_maximum_fusion.1
  14.6 13.4 %all-gather = s32[8,1,33]{2,1,0:T(1,128)S(1)} all-gather(s32[1,1,33]{2,1,0:T(1,128)S(1)} %add_bitcast_fusion), channel_id=1, replica_groups=mesh['seq'=8,'vocab'=4] {'seq'}, dimensions={0}, use_global_device_ids=true | all-gather | bytes 1188 | tf_op jit(solution)/shard_map/all_gather | solution.py:349
  28.5 26.4 %all-gather.3.cloned.1.call-done = bf16[256,6144]{1,0:T(8,128)(2,1)} async-done(((bf16[32,6144]{1,0:T(8,128)(2,1)}), bf16[256,6144]{1,0:T(8,128)(2,1)}) %all-gather.3.cloned.1.call-update) | async-done | bytes 3145744 | tf_op jit(solution)/shard_map/all_gather | solution.py:348
  54.9 2.6 %convolution_convert_fusion = bf16[128,6144]{1,0:T(8,128)(2,1)S(1)} fusion(bf16[256,6144]{1,0:T(8,128)(2,1)} %all-gather.3.cloned.1.call-done, s32[256]{0:T(256)S(1)} %select_n.41), kind=kOutput, calls=%fused_computation.10 | convolution fusion | flops 403472384 | bytes 4719616 | tf_op jit(solution)/shard_map/dot_general | solution.py:360
  57.5 2.5 %fusion.12 = f32[128,768]{1,0:T(8,128)S(1)} fusion(bf16[3,1536,768]{2,1,0:T(8,128)(2,1)} %param.11, bf16[128,6144]{1,0:T(8,128)(2,1)S(1)} %convolution_convert_fusion), kind=kOutput, calls=%fused_computation.15 | convolution fusion | flops 301989888 | bytes 3145728 | tf_op jit(solution)/shard_map/dot_general | solution.py:370
  61.0 1.0 fusion
  62.0 1.1 fusion.40
  63.1 1.1 fusion.37
  64.2 1.1 fusion.34
  65.2 1.3 pad_maximum_fusion
  66.7 0.6 select_reduce_fusion
  67.4 29.4 %reduce-scatter.2.cloned.1.call-done = f32[128,768]{1,0:T(8,128)} async-done(((f32[512,768]{1,0:T(8,128)}), f32[128,768]{1,0:T(8,128)}) %reduce-scatter.2.cloned.1.call-update) | async-done | bytes 393232 | tf_op jit(solution)/shard_map/reduce_scatter | solution.py:373
  96.7 1.1 multiply_reduce_fusion
  97.9 11.7 %all_gather.11.refs_0_ = bf16[512,768]{1,0:T(8,128)(2,1)} all-gather(bf16[128,768]{1,0:T(8,128)(2,1)S(1)} %get-tuple-element.14), channel_id=1, replica_groups=mesh['seq'=8,'vocab'=4] {'vocab'}, dimensions={0}, use_global_device_ids=true | all-gather | bytes 983040 | tf_op jit(solution)/shard_map/all_gather | solution.py:375
  109.6 8.9 %psum.14 = f32[4,128]{1,0:T(4,128)S(1)} all-reduce(f32[4,128]{1,0:T(4,128)S(1)} %broadcast_select_fusion.1), channel_id=1, replica_groups=mesh['seq'=8,'vocab'=4] {'vocab'}, use_global_device_ids=true, to_apply=%region_3.4 | all-reduce | flops 512 | bytes 4096 | tf_op jit(solution)/shard_map/psum | solution.py:384
  118.5 13.6 %psum.15 = f32[4,128]{1,0:T(4,128)S(1)} all-reduce(f32[4,128]{1,0:T(4,128)S(1)} %psum.14), channel_id=1, replica_groups=mesh['seq'=8,'vocab'=4] {'seq'}, use_global_device_ids=true, to_apply=%region_4.5 | all-reduce | flops 512 | bytes 4096 | tf_op jit(solution)/shard_map/psum | solution.py:384
  132.1 0.6 add_rsqrt_fusion
  132.7 72.2 %readout.1 = f32[16,128]{1,0:T(8,128)} custom-call(bf16[512,768]{1,0:T(8,128)(2,1)} %all_gather.11.refs_0_, f32[4,1,128]{2,1,0:T(1,128)} %bitcast.35, s32[1,128]{1,0:T(1,128)} %bitcast.36, bf16[8192,768]{1,0:T(8,128)(2,1)} %refs_3_.1), custom_call_target="tpu_custom_call" | custom-call | tf_op jit(solution)/shard_map/readout/pallas_call | solution.py:280
  204.9 0.7 slice.69
  205.7 0.6 slice.70
  206.2 0.6 copy.18
  (32 shorter events, 2.0 us)
Async XLA Ops:
  7.2 47.7 %all-gather.3.cloned.1.call-start = ((), (), s32[]{:S(2)}) async-start(), calls=%async_computation.1 | async-start | bytes 3538944 | tf_op jit(solution)/shard_map/all_gather | solution.py:348
  9.9 4.6 %copy-start.3 = (s32[1,32]{1,0:T(1,128)S(1)}, s32[1,32]{1,0:T(1,128)}, u32[]{:S(2)}) copy-start(s32[1,32]{1,0:T(1,128)} %param.17) | copy-start | bytes 388
  9.9 18.5 %copy-start = (f32[3,768]{1,0:T(4,128)S(1)}, f32[3,768]{1,0:T(4,128)}, u32[]{:S(2)}) copy-start(f32[3,768]{1,0:T(4,128)} %param.12) | copy-start | bytes 27652
  13.8 82.9 %reduce-scatter.2.cloned.1.call-start = ((), (), s32[]{:S(2)}) async-start(), calls=%async_computation.2 | async-start | bytes 1966080 | tf_op jit(solution)/shard_map/reduce_scatter | solution.py:373
  54.9 5.1 %copy-start.2 = (bf16[3,1536,768]{2,1,0:T(8,128)(2,1)S(1)}, bf16[3,1536,768]{2,1,0:T(8,128)(2,1)}, u32[]{:S(2)}) copy-start(bf16[3,1536,768]{2,1,0:T(8,128)(2,1)} %param.11) | copy-start | bytes 21233668
  66.5 30.3 %copy-start.1 = (f32[768]{0:T(1024)S(1)}, f32[768]{0:T(1024)}, u32[]{:S(2)}) copy-start(f32[768]{0:T(1024)} %param.13) | copy-start | bytes 9220
Sparse Core Ops, SparseCore 0:
  13.9 40.9 all-gather.2
  66.6 30.0 reduce-scatter.1
where the time goes:
time: 214 us
  Pallas kernels  72.2 us (34%)
  waiting for transfers between devices  55.8 us (26%)
  blocking collectives  47.6 us (22%)
  between operations  14.9 us (7%)
  matrix products  10.3 us (5%)
  local copies, waits for them, and re-layouts  7.33 us (3%)
  other arithmetic  5.53 us (3%)
    pallas_call x1, Pallas kernels, readout(): pl.pallas_call(body, out_shape=jax.ShapeDtypeStruct((deep, total), f32),...  72.2 us
    reduce_scatter x1, waiting for transfers between devices, body(): lax.psum_scatter(partial_value, 'vocab', scatter_dimension=0, tiled=True)  29.4 us
    all_gather x1, waiting for transfers between devices, body(): gathered = lax.all_gather(local, 'seq', axis=0, tiled=True)  26.4 us
    psum x2, blocking collectives, body(): every_square = lax.psum(lax.psum(spread, 'vocab'), 'seq').reshape(stacked)  22.5 us
    all_gather x1, blocking collectives, body(): lax.all_gather(jnp.concatenate([answer_count[None, :], targets], axis=1),...  13.4 us
    all_gather x1, blocking collectives, body(): lax.all_gather((lensed * norm_gain[None, :]).astype(bf16), 'vocab', axis=...  11.7 us
  transfers between devices with their start and end apart: 2, of which 2 were waited for; matrix products, arithmetic and copies ran while one was open for 1% of the time, Pallas kernels for 0%

commit v1 on v0

v1 whole, which is shorter than its diff:
```python
import math
import jax
import jax.numpy as jnp
from jax import lax
from jax.experimental import pallas as pl
from jax.experimental.pallas import tpu as pltpu
from jax.sharding import PartitionSpec as P

FLAG_DEV = 16
STATE_MAX, MATRIX_MAX, BIAS_MAX, GAIN_MAX, UNEMBED_MAX = 6.0, 0.078125, 4.0, 1.5, 0.21875
CHUNKS = 4
LAG = 2
SLOTS = 4
LEAD = 3 * CHUNKS
MESH = pl.DeviceIdType.MESH
f32, bf16, i16, i32 = jnp.float32, jnp.bfloat16, jnp.int16, jnp.int32


class Code:
    def __init__(self, model):
        widest = GAIN_MAX * UNEMBED_MAX * model * (STATE_MAX + BIAS_MAX + model * STATE_MAX * MATRIX_MAX)
        self.knee = 7.5e-4
        self.scale = 32700.0 / math.log2(1.0 + 1.02 * widest / self.knee)

    def enc(self, value):
        level = jnp.log2(1.0 + jnp.abs(value) * (1.0 / self.knee)) * self.scale
        return jnp.round(jnp.where(value < 0, -level, level)).astype(i32).astype(i16)

    def dec(self, code):
        level = code.astype(i32).astype(f32)
        size = (jnp.exp2(jnp.abs(level) * (1.0 / self.scale)) - 1.0) * self.knee
        return jnp.where(level < 0, -size, size)


def kernel(
    layers, total, cap, seq_count, vocab_count, model, code,
    probed, final, meta, bias, gain, t_hbm, u_hbm, out_ref,
    u, tr, rows, packed, hit, tgt, spot_col, meta_recv, rs_src, rs_recv, y, sq_part, sq_src, sq_recv, fac,
    own, psend, precv, zsend, zrecv, z3, e3, acc, stat_send, stat_recv, line_send, line_recv,
    u_sem, t_sem, msend_sem, mrecv_sem, rsend_sem, rrecv_sem, fsend_sem, frecv_sem, gsend_sem, grecv_sem,
    ysend_sem, yrecv_sem, qsend_sem, qrecv_sem, vsend_sem, vrecv_sem,
    psend_sem, precv_sem, zsend_sem, zrecv_sem, ssend_sem, srecv_sem, lsend_sem, lrecv_sem,
):
    seq, voc = lax.axis_index("seq"), lax.axis_index("vocab")
    chip, core = seq // 2, seq % 2
    chips = seq_count // 2
    vp, wo = u.shape
    wi = final.shape[1]
    ratio = wi // wo
    half, quarter = vp // 2, vp // 4
    chunk = quarter // CHUNKS
    steps = layers * CHUNKS
    plane = 2 * vocab_count
    share = total // vocab_count
    me = core * vocab_count + voc
    at_end = jnp.logical_or(chip == 0, chip == chips - 1)
    holder = seq // ratio
    holds = holder == voc
    home = (voc * ratio) // 2
    at_home = chip == home

    pieces = 4 * CHUNKS
    piece = vp // pieces

    def u_copy(k):
        part = pl.ds(pl.multiple_of(k * piece, piece), piece)
        return pltpu.make_async_copy(u_hbm.at[part], u.at[part], u_sem.at[k])

    def t_copy(l):
        return pltpu.make_async_copy(t_hbm.at[l], tr.at[l], t_sem.at[l])

    def remote(src, dst, send, recv, device):
        return pltpu.make_async_remote_copy(
            src_ref=src, dst_ref=dst, send_sem=send, recv_sem=recv, device_id=device, device_id_type=MESH
        )

    @pl.loop(0, layers - 1)
    def _(l):
        t_copy(l).start()

    @pl.loop(0, pieces)
    def _(k):
        u_copy(k).start()

    barrier = pltpu.get_barrier_semaphore()

    def in_plane(p):
        q = lax.rem(me + p, plane)
        return q, (chip * 2 + q // vocab_count, lax.rem(q, vocab_count))

    def in_line(p):
        q = lax.rem(chip + p, chips)
        return q, (q * 2 + core, voc)

    def in_column(p):
        q = lax.rem(seq + p, seq_count)
        return q, (q, voc)

    def in_group(p):
        q = lax.rem(voc + p, vocab_count)
        return q, (seq, q)

    partner = (chip * 2 + 1 - core, voc)

    @pl.loop(1, plane)
    def _(p):
        pl.semaphore_signal(barrier, inc=1, device_id=in_plane(p)[1], device_id_type=MESH)

    @pl.loop(1, seq_count)
    def _(p):
        pl.semaphore_signal(barrier, inc=1, device_id=in_column(p)[1], device_id_type=MESH)

    pl.semaphore_wait(barrier, plane - 1 + seq_count - 1)

    def meta_copy(p, slot):
        return remote(meta, meta_recv.at[slot], msend_sem.at[p], mrecv_sem.at[slot], in_column(p)[1])

    @pl.loop(1, seq_count)
    def _(p):
        meta_copy(p, seq).start()

    meta_recv[seq] = meta[...]

    def block(s):
        return pl.ds(pl.multiple_of(s * cap, cap), cap)

    def row_src(i):
        return final if i == 0 else probed.at[i - 1]

    def row_copy(i, p, source):
        src = rows.at[i, block(seq)] if not isinstance(i, int) else row_src(i)
        q, there = in_line(p)
        return remote(
            src, rows.at[i, block(source * 2 + core)], rsend_sem.at[i, p], rrecv_sem.at[i, source], there
        )

    def forward_copy(i, source, other, src=None):
        part = rows.at[i, block(source * 2 + (1 - core if other else core))]
        return remote(part if src is None else src, part, fsend_sem.at[i, source], frecv_sem.at[i, source], partner)

    for i in range(layers):
        if i == 0:
            @pl.loop(1, chips)
            def _(p):
                @pl.when(in_line(p)[0] == home)
                def _():
                    row_copy(0, p, chip).start()

            @pl.when(at_home)
            def _():
                forward_copy(0, chip, False, row_src(0)).start()
        else:
            @pl.loop(1, chips)
            def _(p):
                row_copy(i, p, chip).start()

            forward_copy(i, chip, False, row_src(i)).start()
        rows[i, block(seq), :] = row_src(i)[...]

    acc[...] = jnp.zeros_like(acc)

    def places():
        @pl.loop(1, seq_count)
        def _(p):
            q, _ = in_column(p)
            meta_copy(p, q).wait_recv()

        every = meta_recv[0]
        for q in range(1, seq_count):
            every = every + meta_recv[q]
        slots = seq_count * cap
        lane = lax.broadcasted_iota(i32, (1, slots), 1)
        counts, wanted, starts = every[0:1], every[1:2], every[2:3]
        slot = lane % cap
        place = jnp.where(slot < counts, starts + slot, -1)
        match = (lax.broadcasted_iota(i32, (total, slots), 0) == place).astype(f32).astype(bf16)
        hit[...] = match
        high = wanted // 256
        low = wanted - high * 256
        table = jnp.concatenate(
            [high.astype(f32), low.astype(f32), (place + 1).astype(f32), jnp.zeros((5, slots), f32)], axis=0
        ).astype(bf16)
        names = lax.dot_general(table, match, (((1,), (1,)), ((), ())), preferred_element_type=f32)
        tgt[...] = (names[0:1] * 256.0 + names[1:2]).astype(i32)
        mine = (
            lax.broadcasted_iota(i32, (cap, slots), 0) + seq * cap == lax.broadcasted_iota(i32, (cap, slots), 1)
        ).astype(f32).astype(bf16)
        spots = lax.dot_general(mine, table, (((1,), (1,)), ((), ())), preferred_element_type=f32)
        spot_col[...] = jnp.broadcast_to(spots[:, 2:3] - 1.0, spot_col.shape)

    def wants(i, then):
        pl.when(jnp.logical_or(i > 0, at_home))(then)

    def relay(i):
        def go():
            @pl.loop(1, chips)
            def _(p):
                q, _ = in_line(p)
                row_copy(i, p, q).wait_recv()
                forward_copy(i, q, False).start()

        wants(i, go)

    def part_of(q):
        return pl.ds(pl.multiple_of(q * share, share), share)

    def group_copy(i, p, slot):
        q, there = in_group(p)
        return remote(
            rs_src.at[i, part_of(q)], rs_recv.at[i, slot], gsend_sem.at[i, p], grecv_sem.at[i, slot], there
        )

    def translate(i):
        def go():
            @pl.loop(0, chips)
            def _(q):
                forward_copy(i, q, True).wait_recv()

            packed[...] = jnp.dot(hit[...], rows[i], preferred_element_type=f32).astype(bf16)

            @pl.when(i > 0)
            def _():
                t_copy(i - 1).wait()
                rs_src[i] = jnp.dot(packed[...], tr[i - 1], preferred_element_type=f32)

            @pl.when(holds)
            def _():
                start = pl.multiple_of(lax.rem(seq, ratio) * wo, wo)
                kept = packed[:, pl.ds(start, wo)].astype(f32)

                @pl.when(i > 0)
                def _():
                    rs_src[i] = rs_src[i] + kept

                @pl.when(i == 0)
                def _():
                    rs_src[i] = kept

            @pl.when(jnp.logical_or(i > 0, holds))
            def _():
                @pl.loop(1, vocab_count)
                def _(p):
                    group_copy(i, p, voc).start()

                rs_recv[i, voc] = rs_src[i, part_of(voc), :]

        wants(i, go)

    def y_copy(i, p, owner):
        return remote(
            y.at[i, part_of(owner)], y.at[i, part_of(owner)], ysend_sem.at[i, p], yrecv_sem.at[i, owner],
            in_group(p)[1],
        )

    def sq_copy(i, p, owner):
        return remote(
            sq_part.at[i, owner], sq_part.at[i, owner], qsend_sem.at[i, p], qrecv_sem.at[i, owner], in_group(p)[1]
        )

    def scale(i):
        def go(x):
            y[i, part_of(voc), :] = (x * gain[...]).astype(bf16)
            column = jnp.sum(x * x, axis=1, keepdims=True)
            lane = lax.broadcasted_iota(i32, (share, total), 1)
            row = lax.broadcasted_iota(i32, (share, total), 0) + voc * share
            sq_part[i, voc] = jnp.sum(jnp.where(lane == row, column, 0.0), axis=0, keepdims=True)

            @pl.loop(1, vocab_count)
            def _(p):
                y_copy(i, p, voc).start()

            @pl.loop(1, vocab_count)
            def _(p):
                sq_copy(i, p, voc).start()

        @pl.when(i > 0)
        def _():
            @pl.loop(1, vocab_count)
            def _(p):
                q, _ = in_group(p)
                group_copy(i, p, q).wait_recv()

            x = rs_recv[i, 0]
            for q in range(1, vocab_count):
                x = x + rs_recv[i, q]
            go(x + bias[i - 1])

        @pl.when(i == 0)
        def _():
            @pl.when(jnp.logical_not(holds))
            def _():
                group_copy(0, 1, holder).wait_recv()

            go(rs_recv[0, holder])

    def end_device(e):
        return jnp.where(e < 2, 0, seq_count - 2) + lax.rem(e, 2)

    def v_copy(i, e, source):
        return remote(
            sq_src.at[i], sq_recv.at[i, source], vsend_sem.at[i, e], vrecv_sem.at[i, source], (end_device(e), voc)
        )

    def collect(i):
        @pl.loop(1, vocab_count)
        def _(p):
            q, _ = in_group(p)
            y_copy(i, p, q).wait_recv()
            sq_copy(i, p, q).wait_recv()

        sums = sq_part[i, 0]
        for q in range(1, vocab_count):
            sums = sums + sq_part[i, q]
        sq_src[i] = sums

        @pl.loop(0, 4)
        def _(e):
            @pl.when(end_device(e) != seq)
            def _():
                v_copy(i, e, seq).start()

        @pl.when(at_end)
        def _():
            sq_recv[i, seq] = sums

    def pair_copy(t):
        return remote(
            psend.at[lax.rem(t, SLOTS)], precv.at[t], psend_sem.at[lax.rem(t, SLOTS)], precv_sem.at[t], partner
        )

    def line_copy(k, d):
        to = jnp.minimum(chip + 1, chips - 1) if d == 0 else jnp.maximum(chip - 1, 0)
        return remote(
            zsend.at[k, d], zrecv.at[k, d], zsend_sem.at[k, d], zrecv_sem.at[k, d], (to * 2 + core, voc)
        )

    def rows_at(owner, d, j):
        start = owner * half + d * quarter + j * chunk
        return pl.ds(pl.multiple_of(start, chunk), chunk)

    def product(part, yl):
        return lax.dot_general(u[part, :], yl, (((1,), (1,)), ((), ())), preferred_element_type=f32)

    def fold(value):
        return jnp.sum(value.reshape(chunk // 8, 8, total), axis=0)

    def finish(k, d, value):
        i, j = k // CHUNKS, lax.rem(k, CHUNKS)

        @pl.when(j == 0)
        def _():
            @pl.loop(1, seq_count)
            def _(p):
                q, _ = in_column(p)
                v_copy(i, 0, q).wait_recv()

            squares = sq_recv[i, 0]
            for q in range(1, seq_count):
                squares = squares + sq_recv[i, q]
            fac[i] = lax.rsqrt(squares * (1.0 / model) + 1e-05)

        logit = value * fac[i]
        base = voc * vp + core * half + d * quarter + j * chunk
        spot = lax.broadcasted_iota(i32, (chunk, total), 0) + base
        grown = jnp.exp(logit)
        acc[i] += fold(grown)
        acc[layers + i] += fold(jnp.where(spot == tgt[...], logit, 0.0))

        @pl.when(i == 0)
        def _():
            z3[j] = logit
            e3[j] = grown

        @pl.when(i > 0)
        def _():
            acc[2 * layers + i] += fold(e3[j] * (z3[j] - logit))

    def forward(k, d):
        first = chip == (0 if d == 0 else chips - 1)
        last = chip == (chips - 1 if d == 0 else 0)

        @pl.when(jnp.logical_not(first))
        def _():
            line_copy(k, d).wait_recv()
            own[k, d] = own[k, d] + code.dec(zrecv[k, d])

        @pl.when(jnp.logical_not(last))
        def _():
            zsend[k, d] = code.enc(own[k, d])
            line_copy(k, d).start()

        @pl.when(last)
        def _():
            finish(k, d, own[k, d])

    def stage(t, turn, ahead, then):
        i = t // CHUNKS + ahead

        @pl.when(jnp.logical_and(lax.rem(t, CHUNKS) == turn, jnp.logical_and(i >= 0, i < layers)))
        def _():
            then(i)

    turns = [(CHUNKS * k) // 4 for k in range(4)]

    @pl.loop(LEAD - 2 * CHUNKS - (CHUNKS - turns[3]), LEAD + steps + 1 + LAG * (chips - 1))
    def _(now):
        t = now - LEAD
        stage(now, turns[0], -LEAD // CHUNKS, collect)
        stage(now, turns[3], 3 - LEAD // CHUNKS, relay)
        pl.when(t == turns[3] - 3 * CHUNKS)(places)
        stage(now, turns[1], 2 - LEAD // CHUNKS, translate)
        stage(now, turns[2], 1 - LEAD // CHUNKS, scale)

        @pl.when(jnp.logical_and(t >= 0, t < CHUNKS))
        def _():
            for part in range(4):
                u_copy(part * CHUNKS + t).wait()

        @pl.when(jnp.logical_and(t >= 0, t < steps))
        def _():
            i, j = t // CHUNKS, lax.rem(t, CHUNKS)
            yl = y[i]

            @pl.when(t >= SLOTS)
            def _():
                pair_copy(t - SLOTS).wait_send()

            for d in range(2):
                psend[lax.rem(t, SLOTS), d] = product(rows_at(1 - core, d, j), yl)
            pair_copy(t).start()
            for d in range(2):
                own[t, d] = product(rows_at(core, d, j), yl)

        @pl.when(jnp.logical_and(t >= 1, t <= steps))
        def _():
            pair_copy(t - 1).wait_recv()
            own[t - 1] = own[t - 1] + precv[t - 1]

        for d in range(2):
            k = t - 1 - LAG * (chip if d == 0 else chips - 1 - chip)

            @pl.when(jnp.logical_and(k >= 0, k < steps))
            def _():
                forward(k, d)

    def stat_copy(p, slot):
        return remote(stat_send, stat_recv.at[slot], ssend_sem.at[p], srecv_sem.at[slot], in_plane(p)[1])

    end = jnp.where(chip == 0, 0, 1)

    def line_stat(p, side):
        return remote(line_send, line_recv.at[side], lsend_sem.at[p], lrecv_sem.at[side], in_line(p)[1])

    @pl.when(at_end)
    def _():
        stat = jnp.concatenate(
            [jnp.sum(acc[i], axis=0, keepdims=True) for i in range(3 * layers)]
            + [jnp.zeros((stat_send.shape[0] - 3 * layers, total), f32)] * (stat_send.shape[0] > 3 * layers),
            axis=0,
        )
        stat_send[...] = stat
        stat_recv[me] = stat

        @pl.loop(1, plane)
        def _(p):
            stat_copy(p, me).start()

        @pl.loop(1, plane)
        def _(p):
            stat_copy(p, in_plane(p)[0]).wait_recv()

        full = stat_recv[0]
        for q in range(1, plane):
            full = full + stat_recv[q]
        line_send[...] = full
        line_recv[end] = full

        @pl.loop(1, chips)
        def _(p):
            line_stat(p, end).start()

    @pl.loop(1, seq_count)
    def _(p):
        meta_copy(p, seq).wait_send()

    @pl.loop(0, layers)
    def _(i):
        @pl.loop(1, chips)
        def _(p):
            @pl.when(jnp.logical_or(i > 0, in_line(p)[0] == home))
            def _():
                row_copy(i, p, chip).wait_send()

        @pl.when(jnp.logical_or(i > 0, at_home))
        def _():
            @pl.loop(0, chips)
            def _(q):
                forward_copy(i, q, False).wait_send()

        @pl.loop(1, vocab_count)
        def _(p):
            @pl.when(jnp.logical_or(i > 0, holds))
            def _():
                group_copy(i, p, voc).wait_send()

            y_copy(i, p, voc).wait_send()
            sq_copy(i, p, voc).wait_send()

        @pl.loop(0, 4)
        def _(e):
            @pl.when(end_device(e) != seq)
            def _():
                v_copy(i, e, seq).wait_send()

    @pl.loop(steps - SLOTS, steps)
    def _(t):
        pair_copy(t).wait_send()

    @pl.loop(0, steps)
    def _(k):
        for d in range(2):
            @pl.when(chip != (chips - 1 if d == 0 else 0))
            def _():
                line_copy(k, d).wait_send()

    @pl.when(at_end)
    def _():
        @pl.loop(1, plane)
        def _(p):
            stat_copy(p, me).wait_send()

        @pl.loop(1, chips)
        def _(p):
            line_stat(p, end).wait_send()

    for side in range(2):
        @pl.when(chip != (0 if side == 0 else chips - 1))
        def _():
            line_stat(1, side).wait_recv()

    full = line_recv[0] + line_recv[1]
    total_exp, picked = full[:layers], full[layers : 2 * layers]
    cross = full[2 * layers + 1 : 3 * layers]
    log_total = jnp.log(total_exp)
    result = [picked[l : l + 1] - log_total[l : l + 1] for l in list(range(1, layers)) + [0]]
    for l in range(1, layers):
        result.append(cross[l - 1 : l] / total_exp[0:1] - log_total[0:1] + log_total[l : l + 1])
    lane = lax.broadcasted_iota(i32, (cap, total), 1).astype(f32)
    owned = lane == spot_col[...]
    place = lax.broadcasted_iota(i32, out_ref.shape, 1)
    out = jnp.zeros(out_ref.shape, f32)
    for l, value in enumerate(result):
        column = jnp.sum(jnp.where(owned, value, 0.0), axis=1, keepdims=True)
        out = jnp.where(place == l, column, out)
    out_ref[...] = out


def readout(probed, final, meta, bias, gain, translator, unembed, seq_count, vocab_count, cap, total, model):
    layers = probed.shape[0] + 1
    vp, wo = unembed.shape
    wi = final.shape[1]
    steps = layers * CHUNKS
    chunk = vp // 4 // CHUNKS
    plane, chips = 2 * vocab_count, seq_count // 2
    share = total // vocab_count
    code = Code(model)
    deep = -(-3 * layers // 8) * 8
    dma = pltpu.SemaphoreType.DMA
    vmem = pl.BlockSpec(memory_space=pltpu.VMEM)
    hbm = pl.BlockSpec(memory_space=pl.ANY)
    body = lambda *refs: kernel(layers, total, cap, seq_count, vocab_count, model, code, *refs)
    return pl.pallas_call(
        body,
        out_shape=jax.ShapeDtypeStruct((cap, 128), f32),
        in_specs=[vmem] * 5 + [hbm, hbm],
        out_specs=vmem,
        scratch_shapes=[
            pltpu.VMEM((vp, wo), bf16),
            pltpu.VMEM((layers - 1, wi, wo), bf16),
            pltpu.VMEM((layers, seq_count * cap, wi), bf16),
            pltpu.VMEM((total, wi), bf16),
            pltpu.VMEM((total, seq_count * cap), bf16),
            pltpu.VMEM((1, total), i32),
            pltpu.VMEM((cap, total), f32),
            pltpu.VMEM((seq_count, 8, seq_count * cap), i32),
            pltpu.VMEM((layers, total, wo), f32),
            pltpu.VMEM((layers, vocab_count, share, wo), f32),
            pltpu.VMEM((layers, total, wo), bf16),
            pltpu.VMEM((layers, vocab_count, 1, total), f32),
            pltpu.VMEM((layers, 1, total), f32),
            pltpu.VMEM((layers, seq_count, 1, total), f32),
            pltpu.VMEM((layers, 1, total), f32),
            pltpu.VMEM((steps, 2, chunk, total), f32),
            pltpu.VMEM((SLOTS, 2, chunk, total), f32),
            pltpu.VMEM((steps, 2, chunk, total), f32),
            pltpu.VMEM((steps, 2, chunk, total), i16),
            pltpu.VMEM((steps, 2, chunk, total), i16),
            pltpu.VMEM((CHUNKS, chunk, total), f32),
            pltpu.VMEM((CHUNKS, chunk, total), f32),
            pltpu.VMEM((3 * layers, 8, total), f32),
            pltpu.VMEM((deep, total), f32),
            pltpu.VMEM((plane, deep, total), f32),
            pltpu.VMEM((deep, total), f32),
            pltpu.VMEM((2, deep, total), f32),
            dma((4 * CHUNKS,)),
            dma((layers - 1,)),
            dma((seq_count,)),
            dma((seq_count,)),
            dma((layers, chips)),
            dma((layers, chips)),
            dma((layers, chips)),
            dma((layers, chips)),
            dma((layers, vocab_count)),
            dma((layers, vocab_count)),
            dma((layers, vocab_count)),
            dma((layers, vocab_count)),
            dma((layers, vocab_count)),
            dma((layers, vocab_count)),
            dma((layers, 4)),
            dma((layers, seq_count)),
            dma((SLOTS,)),
            dma((steps,)),
            dma((steps, 2)),
            dma((steps, 2)),
            dma((plane,)),
            dma((plane,)),
            dma((chips,)),
            dma((2,)),
        ],
        compiler_params=pltpu.CompilerParams(
            collective_id=0, has_side_effects=True, vmem_limit_bytes=63 << 20
        ),
        name="readout",
    )(probed, final, meta, bias, gain, translator, unembed)


def body(
    probe_states,
    final_states,
    translator,
    translator_bias,
    norm_gain,
    unembed,
    answer_rows,
    answer_count,
    targets,
):
    seq_count = lax.axis_size("seq")
    vocab_count = lax.axis_size("vocab")
    seq_index = lax.axis_index("seq")
    layers = probe_states.shape[0]
    cap = answer_rows.shape[1]
    model = probe_states.shape[2] * vocab_count
    picks = answer_rows[0]

    probed = jnp.take(probe_states, picks, axis=1, mode="clip")
    final = jnp.take(final_states, picks, axis=0, mode="clip")
    lane = jnp.arange(seq_count * cap, dtype=i32)[None, :]
    line = jnp.arange(8, dtype=i32)[:, None]
    mine = lane // cap == seq_index
    after = lane // cap > seq_index
    meta = jnp.where(jnp.logical_and(line == 0, mine), answer_count[0], 0)
    meta = jnp.where(jnp.logical_and(line == 1, mine), jnp.tile(targets, (1, seq_count)), meta)
    meta = jnp.where(jnp.logical_and(line == 2, after), answer_count[0], meta)

    out = readout(
        probed,
        final,
        meta,
        translator_bias[:, None, :],
        norm_gain[None, :],
        translator,
        unembed,
        seq_count,
        vocab_count,
        cap,
        seq_count * FLAG_DEV,
        model,
    )
    flat = out[:, : 2 * layers + 1].T
    return (flat[: layers + 1, None, :], flat[layers + 1 :, None, :])


def solution(mesh):
    in_specs = (
        P(None, "seq", "vocab"),
        P("seq", "vocab"),
        P(None, "vocab", "seq"),
        P(None, "seq"),
        P("seq"),
        P("vocab", "seq"),
        P("seq", None),
        P("seq"),
        P("seq", None),
    )
    out_specs = (P(None, "seq", None), P(None, "seq", None))
    return jax.shard_map(body, mesh=mesh, in_specs=in_specs, out_specs=out_specs, check_vma=False)
```

time: 214 us -> 128 us (0.60)
  waiting for transfers between devices: 55.8 us -> 0 us
  blocking collectives: 47.6 us -> 0 us
  Pallas kernels: 72.2 us -> 113 us
  between operations: 14.9 us -> 1.31 us
  matrix products: 10.3 us -> 0 us
  local copies, waits for them, and re-layouts: 7.33 us -> 11.8 us
  other arithmetic: 5.53 us -> 1.35 us
    pallas_call x1, Pallas kernels: 72.2 us -> 113 us  [readout(): pl.pallas_call(body, out_shape=jax.ShapeDtypeStruct((cap, 128), f32), in_...]
    reduce_scatter x1 -> x0, waiting for transfers between devices: 29.4 us -> none  [body(): lax.psum_scatter(partial_value, 'vocab', scatter_dimension=0, tiled=True)]
    all_gather x1 -> x0, waiting for transfers between devices: 26.4 us -> none  [body(): gathered = lax.all_gather(local, 'seq', axis=0, tiled=True)]
    all_gather x2 -> x0, blocking collectives: 25.1 us -> none  [the longest x1 13.4 us: body(): lax.all_gather(jnp.concatenate([answer_count[None, :], targets], axis=1),...]
    psum x2 -> x0, blocking collectives: 22.5 us -> none  [body(): every_square = lax.psum(lax.psum(spread, 'vocab'), 'seq').reshape(stacked)]
    dot_general x8 -> x0, matrix products: 10.3 us -> none  [the longest x4 4.19 us: body(): piece = jnp.dot(parts[l], identity, preferred_element_type=f32)]
    broadcast_in_dim x2 -> x4, local copies, waits for them, and re-layouts: 0.08 us -> 2.67 us  [the longest x1 1.31 us: body(): translator_bias[:, None, :]]
  transfers between devices with their start and end apart: 2 -> 0, of which waited for: 2 -> 0; matrix products, arithmetic and copies ran while one was open for 1% -> 0% of each run, Pallas kernels for 0% -> 0%
where the time goes in v1:
time: 128 us; the launch traced here: 127 us
  Pallas kernels  113 us (88%)
  local copies, waits for them, and re-layouts  11.8 us (9%)
  other arithmetic  1.35 us (1%)
  between operations  1.31 us (1%)
    pallas_call x1, Pallas kernels, readout(): pl.pallas_call(body, out_shape=jax.ShapeDtypeStruct((cap, 128), f32), in_...  113 us
    gather x1, local copies, waits for them, and re-layouts, body(): final = jnp.take(final_states, picks, axis=0, mode='clip')  3.65 us
    gather x1, local copies, waits for them, and re-layouts, body(): probed = jnp.take(probe_states, picks, axis=1, mode='clip')  2.76 us

profile of v1, /device:TPU:0, one launch (start us, length us, event | category | flops | bytes accessed | tf_op | source)
XLA Modules:
  0.0 127.4 jit_solution(11600505001951468443)
XLA Ops:
  1.3 1.3 %broadcast_in_dim.43.refs_4_ = f32[1,768]{1,0:T(1,128)} reshape(f32[768]{0:T(1024)} %param.13) | data formatting | bytes 6144 | tf_op jit(solution)/shard_map/broadcast_in_dim | solution.py:671
  2.6 0.7 pad_clamp_fusion
  3.3 0.7 tile.12
  3.9 0.1 tile.13
  4.0 0.7 select_select_fusion.refs_2_
  4.7 1.3 %broadcast_in_dim.42.refs_3_ = f32[3,1,768]{2,1,0:T(1,128)} reshape(f32[3,768]{1,0:T(4,128)} %param.12) | data formatting | bytes 18432 | tf_op jit(solution)/shard_map/broadcast_in_dim | solution.py:670
  6.0 3.7 %gather_fusion.1 = bf16[32,1536]{1,0:T(8,128)(2,1)} fusion(bf16[1024,1536]{1,0:T(8,128)(2,1)} %param.10, s32[1024]{0:T(1024)S(1)} %pad_clamp_fusion), kind=kCustom, calls=%fused_computation.1 | custom fusion | bytes 196736 | tf_op jit(solution)/shard_map/jit(_take)/gather | solution.py:657
  9.6 2.8 %gather_fusion = bf16[32,3,1536]{2,0,1:T(8,128)(2,1)} fusion(bf16[3,1024,1536]{2,1,0:T(8,128)(2,1)} %param.9, s32[1024]{0:T(1024)S(1)} %pad_clamp_fusion), kind=kCustom, calls=%fused_computation | custom fusion | bytes 589952 | tf_op jit(solution)/shard_map/jit(_take)/gather | solution.py:656
  12.4 112.9 %readout.1 = f32[32,128]{1,0:T(8,128)} custom-call(bf16[3,32,1536]{2,1,0:T(8,128)(2,1)} %bitcast.11, bf16[32,1536]{1,0:T(8,128)(2,1)} %gather_fusion.1, s32[8,256]{1,0:T(8,128)} %select_select_fusion.refs_2_, f32[3,1,768]{2,1,0:T(1,128)} %broadcast_in_dim.42.refs_3_, f32[1,768]{1,0:T(1,128)} %broadcast_in_dim.43.refs_4_, bf16[3,1536,768]{2,1,0:T(8,128)(2,1)} %refs_5_.1, ...), custom_call_target="tpu_custom_call" | custom-call | tf_op jit(solution)/shard_map/readout/pallas_call | solution.py:572
  125.3 0.7 slice_bitcast_fusion.2
  126.1 0.1 slice_bitcast_fusion
  126.1 0.6 copy.18
  126.8 0.7 copy.17
  (4 shorter events, 0.0 us)

commit v2 on v1

--- a/solution.py
+++ b/solution.py
@@ -11,14 +11,14 @@
 CHUNKS = 4
 LAG = 2
 SLOTS = 4
+PACK = 8
 LEAD = 3 * CHUNKS
 MESH = pl.DeviceIdType.MESH
 f32, bf16, i16, i32 = jnp.float32, jnp.bfloat16, jnp.int16, jnp.int32
 
 
 class Code:
-    def __init__(self, model):
-        widest = GAIN_MAX * UNEMBED_MAX * model * (STATE_MAX + BIAS_MAX + model * STATE_MAX * MATRIX_MAX)
+    def __init__(self, widest):
         self.knee = 7.5e-4
         self.scale = 32700.0 / math.log2(1.0 + 1.02 * widest / self.knee)
 
@@ -33,9 +33,9 @@
 
 
 def kernel(
-    layers, total, cap, seq_count, vocab_count, model, code,
-    probed, final, meta, bias, gain, t_hbm, u_hbm, out_ref,
-    u, tr, rows, packed, hit, tgt, spot_col, meta_recv, rs_src, rs_recv, y, sq_part, sq_src, sq_recv, fac,
+    layers, total, cap, seq_count, vocab_count, model, code, xcode,
+    picked_rows, count, wanted_ref, bias, gain, t_hbm, u_hbm, prob_ref, kl_ref,
+    u, tr, meta, rows, packed, hit, tgt, spot_col, meta_recv, part, rs_own, rs_src, rs_recv, y, sq_part, sq_src, sq_recv, fac,
     own, psend, precv, zsend, zrecv, z3, e3, acc, stat_send, stat_recv, line_send, line_recv,
     u_sem, t_sem, msend_sem, mrecv_sem, rsend_sem, rrecv_sem, fsend_sem, frecv_sem, gsend_sem, grecv_sem,
     ysend_sem, yrecv_sem, qsend_sem, qrecv_sem, vsend_sem, vrecv_sem,
@@ -45,7 +45,7 @@
     chip, core = seq // 2, seq % 2
     chips = seq_count // 2
     vp, wo = u.shape
-    wi = final.shape[1]
+    wi = picked_rows.shape[2]
     ratio = wi // wo
     half, quarter = vp // 2, vp // 4
     chunk = quarter // CHUNKS
@@ -74,6 +74,9 @@
             src_ref=src, dst_ref=dst, send_sem=send, recv_sem=recv, device_id=device, device_id_type=MESH
         )
 
+    meta[...] = jnp.full(meta.shape, count[0], i32)
+    meta[:, :cap] = wanted_ref[...]
+
     @pl.loop(0, layers - 1)
     def _(l):
         t_copy(l).start()
@@ -110,7 +113,8 @@
     def _(p):
         pl.semaphore_signal(barrier, inc=1, device_id=in_column(p)[1], device_id_type=MESH)
 
-    pl.semaphore_wait(barrier, plane - 1 + seq_count - 1)
+    with jax.named_scope('barrier'):
+        pl.semaphore_wait(barrier, plane - 1 + seq_count - 1)
 
     def meta_copy(p, slot):
         return remote(meta, meta_recv.at[slot], msend_sem.at[p], mrecv_sem.at[slot], in_column(p)[1])
@@ -125,38 +129,50 @@
         return pl.ds(pl.multiple_of(s * cap, cap), cap)
 
     def row_src(i):
-        return final if i == 0 else probed.at[i - 1]
-
-    def row_copy(i, p, source):
-        src = rows.at[i, block(seq)] if not isinstance(i, int) else row_src(i)
-        q, there = in_line(p)
+        return picked_rows.at[i]
+
+    def row_copy(i, source, d, src=None):
+        to = jnp.minimum(chip + 1, chips - 1) if d == 0 else jnp.maximum(chip - 1, 0)
+        here = rows.at[i, block(source * 2 + core)]
         return remote(
-            src, rows.at[i, block(source * 2 + core)], rsend_sem.at[i, p], rrecv_sem.at[i, source], there
-        )
+            here if src is None else src, here, rsend_sem.at[i, source, d], rrecv_sem.at[i, source], (to * 2 + core, voc)
+        )
+
+    def passes(d):
+        return chip < chips - 1 if d == 0 else chip > 0
+
+    def home_copy(source):
+        here = rows.at[0, block(source * 2 + core)]
+        return remote(picked_rows.at[0], here, rsend_sem.at[0, chip, 0], rrecv_sem.at[0, source], (home * 2 + core, voc))
 
     def forward_copy(i, source, other, src=None):
         part = rows.at[i, block(source * 2 + (1 - core if other else core))]
         return remote(part if src is None else src, part, fsend_sem.at[i, source], frecv_sem.at[i, source], partner)
 
+    def depart(i):
+        for d in range(2):
+            @pl.when(passes(d))
+            def _():
+                row_copy(i, chip, d, row_src(i)).start()
+
+        forward_copy(i, chip, False, row_src(i)).start()
+
+    @pl.when(at_home)
+    def _():
+        forward_copy(0, chip, False, picked_rows.at[0]).start()
+
+    @pl.when(jnp.logical_not(at_home))
+    def _():
+        home_copy(chip).start()
+
     for i in range(layers):
-        if i == 0:
-            @pl.loop(1, chips)
-            def _(p):
-                @pl.when(in_line(p)[0] == home)
-                def _():
-                    row_copy(0, p, chip).start()
-
-            @pl.when(at_home)
-            def _():
-                forward_copy(0, chip, False, row_src(0)).start()
-        else:
-            @pl.loop(1, chips)
-            def _(p):
-                row_copy(i, p, chip).start()
-
-            forward_copy(i, chip, False, row_src(i)).start()
         rows[i, block(seq), :] = row_src(i)[...]
 
+    @pl.when(jnp.logical_not(at_home))
+    def _():
+        home_copy(chip).wait_send()
+
+    depart(1)
     acc[...] = jnp.zeros_like(acc)
 
     def places():
@@ -165,20 +181,31 @@
             q, _ = in_column(p)
             meta_copy(p, q).wait_recv()
 
-        every = meta_recv[0]
-        for q in range(1, seq_count):
-            every = every + meta_recv[q]
+        every = jnp.concatenate([meta_recv[q] for q in range(seq_count)], axis=0)
         slots = seq_count * cap
         lane = lax.broadcasted_iota(i32, (1, slots), 1)
-        counts, wanted, starts = every[0:1], every[1:2], every[2:3]
+        owner = lax.broadcasted_iota(i32, (seq_count, slots), 1) // cap
+        row = lax.broadcasted_iota(i32, (seq_count, slots), 0)
+        counted = jnp.broadcast_to(every[:, cap : cap + 1], (seq_count, slots))
+        counts = jnp.sum(jnp.where(row == owner, counted, 0), axis=0, keepdims=True)
+        starts = jnp.sum(jnp.where(row < owner, counted, 0), axis=0, keepdims=True)
+        wide = every.shape[1]
+        spread = (
+            lax.broadcasted_iota(i32, (wide, slots), 0) == lax.broadcasted_iota(i32, (wide, slots), 1) % cap
+        ).astype(f32).astype(bf16)
+        high = every // 256
+        low = every - high * 256
+
+        def lanes(byte):
+            laid = jnp.dot(byte.astype(f32).astype(bf16), spread, preferred_element_type=f32)
+            return jnp.sum(jnp.where(row == owner, laid, 0.0), axis=0, keepdims=True)
+
         slot = lane % cap
         place = jnp.where(slot < counts, starts + slot, -1)
         match = (lax.broadcasted_iota(i32, (total, slots), 0) == place).astype(f32).astype(bf16)
         hit[...] = match
-        high = wanted // 256
-        low = wanted - high * 256
         table = jnp.concatenate(
-            [high.astype(f32), low.astype(f32), (place + 1).astype(f32), jnp.zeros((5, slots), f32)], axis=0
+            [lanes(high), lanes(low), (place + 1).astype(f32), jnp.zeros((5, slots), f32)], axis=0
         ).astype(bf16)
         names = lax.dot_general(table, match, (((1,), (1,)), ((), ())), preferred_element_type=f32)
         tgt[...] = (names[0:1] * 256.0 + names[1:2]).astype(i32)
@@ -191,15 +218,43 @@
     def wants(i, then):
         pl.when(jnp.logical_or(i > 0, at_home))(then)
 
+    def gather_home():
+        @pl.loop(1, chips)
+        def _(p):
+            q, _ = in_line(p)
+            home_copy(q).wait_recv()
+            forward_copy(0, q, False).start()
+
     def relay(i):
-        def go():
-            @pl.loop(1, chips)
-            def _(p):
-                q, _ = in_line(p)
-                row_copy(i, p, q).wait_recv()
-                forward_copy(i, q, False).start()
-
-        wants(i, go)
+        @pl.loop(1, chips)
+        def _(p):
+            for d in range(2):
+                source = chip - p if d == 0 else chip + p
+
+                @pl.when(source >= 0 if d == 0 else source < chips)
+                def _():
+                    row_copy(i, source, d).wait_recv()
+
+                    @pl.when(passes(d))
+                    def _():
+                        row_copy(i, source, d).start()
+
+                    forward_copy(i, source, False).start()
+
+    def early(i):
+        pl.when(jnp.logical_and(i == 0, at_home))(gather_home)
+
+        @pl.when(jnp.logical_and(i > 0, jnp.logical_not(at_end)))
+        def _():
+            relay(i)
+
+        for later in range(2, layers):
+            pl.when(i == later - 2)(lambda: depart(later))
+
+    def late(i):
+        @pl.when(jnp.logical_and(i > 0, at_end))
+        def _():
+            relay(i)
 
     def part_of(q):
         return pl.ds(pl.multiple_of(q * share, share), share)
@@ -221,7 +276,7 @@
             @pl.when(i > 0)
             def _():
                 t_copy(i - 1).wait()
-                rs_src[i] = jnp.dot(packed[...], tr[i - 1], preferred_element_type=f32)
+                part[...] = jnp.dot(packed[...], tr[i - 1], preferred_element_type=f32)
 
             @pl.when(holds)
             def _():
@@ -230,19 +285,21 @@
 
                 @pl.when(i > 0)
                 def _():
-                    rs_src[i] = rs_src[i] + kept
+                    part[...] = part[...] + kept
 
                 @pl.when(i == 0)
                 def _():
-                    rs_src[i] = kept
+                    part[...] = kept
 
             @pl.when(jnp.logical_or(i > 0, holds))
             def _():
+                rs_src[i] = xcode.enc(part[...])
+
                 @pl.loop(1, vocab_count)
                 def _(p):
                     group_copy(i, p, voc).start()
 
-                rs_recv[i, voc] = rs_src[i, part_of(voc), :]
+                rs_own[i] = part[part_of(voc), :]
 
         wants(i, go)
 
@@ -259,7 +316,7 @@
 
     def scale(i):
         def go(x):
-            y[i, part_of(voc), :] = (x * gain[...]).astype(bf16)
+            y[i, part_of(voc), :] = (x * gain[...].reshape(1, wo)).astype(bf16)
             column = jnp.sum(x * x, axis=1, keepdims=True)
             lane = lax.broadcasted_iota(i32, (share, total), 1)
             row = lax.broadcasted_iota(i32, (share, total), 0) + voc * share
@@ -275,23 +332,21 @@
 
         @pl.when(i > 0)
         def _():
-            @pl.loop(1, vocab_count)
-            def _(p):
+            x = rs_own[i] + bias[pl.ds(i - 1, 1), :]
+            for p in range(1, vocab_count):
                 q, _ = in_group(p)
                 group_copy(i, p, q).wait_recv()
-
-            x = rs_recv[i, 0]
-            for q in range(1, vocab_count):
-                x = x + rs_recv[i, q]
-            go(x + bias[i - 1])
-
-        @pl.when(i == 0)
-        def _():
-            @pl.when(jnp.logical_not(holds))
-            def _():
-                group_copy(0, 1, holder).wait_recv()
-
-            go(rs_recv[0, holder])
+                x = x + xcode.dec(rs_recv[i, q])
+            go(x)
+
+        @pl.when(jnp.logical_and(i == 0, holds))
+        def _():
+            go(rs_own[0])
+
+        @pl.when(jnp.logical_and(i == 0, jnp.logical_not(holds)))
+        def _():
+            group_copy(0, 1, holder).wait_recv()
+            go(xcode.dec(rs_recv[0, holder]))
 
     def end_device(e):
         return jnp.where(e < 2, 0, seq_count - 2) + lax.rem(e, 2)
@@ -381,7 +436,8 @@
 
         @pl.when(jnp.logical_not(first))
         def _():
-            line_copy(k, d).wait_recv()
+            with jax.named_scope('linewait'):
+                line_copy(k, d).wait_recv()
             own[k, d] = own[k, d] + code.dec(zrecv[k, d])
 
         @pl.when(jnp.logical_not(last))
@@ -398,7 +454,8 @@
 
         @pl.when(jnp.logical_and(lax.rem(t, CHUNKS) == turn, jnp.logical_and(i >= 0, i < layers)))
         def _():
-            then(i)
+            with jax.named_scope(then.__name__):
+                then(i)
 
     turns = [(CHUNKS * k) // 4 for k in range(4)]
 
@@ -406,10 +463,11 @@
     def _(now):
         t = now - LEAD
         stage(now, turns[0], -LEAD // CHUNKS, collect)
-        stage(now, turns[3], 3 - LEAD // CHUNKS, relay)
+        stage(now, turns[3], 3 - LEAD // CHUNKS, early)
         pl.when(t == turns[3] - 3 * CHUNKS)(places)
-        stage(now, turns[1], 2 - LEAD // CHUNKS, translate)
-        stage(now, turns[2], 1 - LEAD // CHUNKS, scale)
+        stage(now, turns[1], 1 - LEAD // CHUNKS, scale)
+        stage(now, turns[2], 2 - LEAD // CHUNKS, late)
+        stage(now, turns[2], 2 - LEAD // CHUNKS, translate)
 
         @pl.when(jnp.logical_and(t >= 0, t < CHUNKS))
         def _():
@@ -420,6 +478,7 @@
         def _():
             i, j = t // CHUNKS, lax.rem(t, CHUNKS)
             yl = y[i]
+            scope = jax.named_scope('dots'); scope.__enter__()
 
             @pl.when(t >= SLOTS)
             def _():
@@ -430,18 +489,21 @@
             pair_copy(t).start()
             for d in range(2):
                 own[t, d] = product(rows_at(core, d, j), yl)
+            scope.__exit__(None, None, None)
 
         @pl.when(jnp.logical_and(t >= 1, t <= steps))
         def _():
-            pair_copy(t - 1).wait_recv()
-            own[t - 1] = own[t - 1] + precv[t - 1]
+            with jax.named_scope('pairsum'):
+                pair_copy(t - 1).wait_recv()
+                own[t - 1] = own[t - 1] + precv[t - 1]
 
         for d in range(2):
             k = t - 1 - LAG * (chip if d == 0 else chips - 1 - chip)
 
             @pl.when(jnp.logical_and(k >= 0, k < steps))
             def _():
-                forward(k, d)
+                with jax.named_scope('fwd%d' % d):
+                    forward(k, d)
 
     def stat_copy(p, slot):
         return remote(stat_send, stat_recv.at[slot], ssend_sem.at[p], srecv_sem.at[slot], in_plane(p)[1])
@@ -465,9 +527,10 @@
         def _(p):
             stat_copy(p, me).start()
 
-        @pl.loop(1, plane)
-        def _(p):
-            stat_copy(p, in_plane(p)[0]).wait_recv()
+        with jax.named_scope('planewait'):
+            @pl.loop(1, plane)
+            def _(p):
+                stat_copy(p, in_plane(p)[0]).wait_recv()
 
         full = stat_recv[0]
         for q in range(1, plane):
@@ -485,11 +548,12 @@
 
     @pl.loop(0, layers)
     def _(i):
-        @pl.loop(1, chips)
-        def _(p):
-            @pl.when(jnp.logical_or(i > 0, in_line(p)[0] == home))
-            def _():
-                row_copy(i, p, chip).wait_send()
+        @pl.loop(0, chips)
+        def _(q):
+            for d in range(2):
+                @pl.when(jnp.logical_and(jnp.logical_and(i > 0, passes(d)), q <= chip if d == 0 else q >= chip))
+                def _():
+                    row_copy(i, q, d).wait_send()
 
         @pl.when(jnp.logical_or(i > 0, at_home))
         def _():
@@ -536,8 +600,10 @@
     for side in range(2):
         @pl.when(chip != (0 if side == 0 else chips - 1))
         def _():
-            line_stat(1, side).wait_recv()
-
+            with jax.named_scope('statwait'):
+                line_stat(1, side).wait_recv()
+
+    scope2 = jax.named_scope('final'); scope2.__enter__()
     full = line_recv[0] + line_recv[1]
     total_exp, picked = full[:layers], full[layers : 2 * layers]
     cross = full[2 * layers + 1 : 3 * layers]
@@ -547,44 +613,87 @@
         result.append(cross[l - 1 : l] / total_exp[0:1] - log_total[0:1] + log_total[l : l + 1])
     lane = lax.broadcasted_iota(i32, (cap, total), 1).astype(f32)
     owned = lane == spot_col[...]
-    place = lax.broadcasted_iota(i32, out_ref.shape, 1)
-    out = jnp.zeros(out_ref.shape, f32)
+    place = lax.broadcasted_iota(i32, (cap, 128), 1)
+    out = jnp.zeros((cap, 128), f32)
     for l, value in enumerate(result):
         column = jnp.sum(jnp.where(owned, value, 0.0), axis=1, keepdims=True)
         out = jnp.where(place == l, column, out)
-    out_ref[...] = out
-
-
-def readout(probed, final, meta, bias, gain, translator, unembed, seq_count, vocab_count, cap, total, model):
-    layers = probed.shape[0] + 1
+    turned = out.T
+    for l in range(layers):
+        prob_ref[l] = turned[l : l + 1]
+    for l in range(layers - 1):
+        kl_ref[l] = turned[layers + l : layers + l + 1]
+    scope2.__exit__(None, None, None)
+
+
+def pick_kernel(layers, cap, picks, probe_hbm, final_hbm, out_ref, found, sem):
+    @pl.loop(0, cap)
+    def _(k):
+        first = pl.ds(pl.multiple_of(picks[0, k] // PACK * PACK, PACK), PACK)
+        spot = pl.ds(pl.multiple_of(k * PACK, PACK), PACK)
+        pltpu.make_async_copy(final_hbm.at[first], found.at[0, spot], sem.at[0]).start()
+        for l in range(1, layers):
+            pltpu.make_async_copy(probe_hbm.at[l - 1, first], found.at[l, spot], sem.at[l]).start()
+
+    row = lax.broadcasted_iota(i32, (cap, cap * PACK), 0)
+    wants = jnp.zeros((cap, cap * PACK), i32)
+    for k in range(cap):
+        wants = jnp.where(row == k, k * PACK + picks[0, k] % PACK, wants)
+    match = (lax.broadcasted_iota(i32, (cap, cap * PACK), 1) == wants).astype(f32).astype(bf16)
+    for l in range(layers):
+        pltpu.make_async_copy(found.at[l], found.at[l], sem.at[l]).wait()
+        out_ref[l] = jnp.dot(match, found[l], preferred_element_type=f32).astype(bf16)
+
+
+def pick(answer_rows, probe_states, final_states):
+    layers, cap, wi = probe_states.shape[0] + 1, answer_rows.shape[1], final_states.shape[1]
+    hbm = pl.BlockSpec(memory_space=pl.ANY)
+    return pl.pallas_call(
+        lambda *refs: pick_kernel(layers, cap, *refs),
+        out_shape=jax.ShapeDtypeStruct((layers, cap, wi), bf16),
+        in_specs=[pl.BlockSpec(memory_space=pltpu.SMEM), hbm, hbm],
+        out_specs=pl.BlockSpec(memory_space=pltpu.VMEM),
+        scratch_shapes=[pltpu.VMEM((layers, cap * PACK, wi), bf16), pltpu.SemaphoreType.DMA((layers,))],
+        name="pick",
+    )(answer_rows, probe_states, final_states)
+
+
+def readout(rows, count, wanted, bias, gain, translator, unembed, seq_count, vocab_count, total, model):
+    layers, cap, wi = rows.shape
     vp, wo = unembed.shape
-    wi = final.shape[1]
     steps = layers * CHUNKS
     chunk = vp // 4 // CHUNKS
     plane, chips = 2 * vocab_count, seq_count // 2
     share = total // vocab_count
-    code = Code(model)
+    code = Code(GAIN_MAX * UNEMBED_MAX * model * (STATE_MAX + BIAS_MAX + model * STATE_MAX * MATRIX_MAX))
+    xcode = Code(STATE_MAX + BIAS_MAX + model * STATE_MAX * MATRIX_MAX)
     deep = -(-3 * layers // 8) * 8
     dma = pltpu.SemaphoreType.DMA
     vmem = pl.BlockSpec(memory_space=pltpu.VMEM)
     hbm = pl.BlockSpec(memory_space=pl.ANY)
-    body = lambda *refs: kernel(layers, total, cap, seq_count, vocab_count, model, code, *refs)
+    body = lambda *refs: kernel(layers, total, cap, seq_count, vocab_count, model, code, xcode, *refs)
     return pl.pallas_call(
         body,
-        out_shape=jax.ShapeDtypeStruct((cap, 128), f32),
-        in_specs=[vmem] * 5 + [hbm, hbm],
-        out_specs=vmem,
+        out_shape=(
+            jax.ShapeDtypeStruct((layers, 1, cap), f32),
+            jax.ShapeDtypeStruct((layers - 1, 1, cap), f32),
+        ),
+        in_specs=[vmem, pl.BlockSpec(memory_space=pltpu.SMEM), vmem, vmem, vmem, hbm, hbm],
+        out_specs=(vmem, vmem),
         scratch_shapes=[
             pltpu.VMEM((vp, wo), bf16),
             pltpu.VMEM((layers - 1, wi, wo), bf16),
+            pltpu.VMEM((1, 128), i32),
             pltpu.VMEM((layers, seq_count * cap, wi), bf16),
             pltpu.VMEM((total, wi), bf16),
             pltpu.VMEM((total, seq_count * cap), bf16),
             pltpu.VMEM((1, total), i32),
             pltpu.VMEM((cap, total), f32),
-            pltpu.VMEM((seq_count, 8, seq_count * cap), i32),
-            pltpu.VMEM((layers, total, wo), f32),
-            pltpu.VMEM((layers, vocab_count, share, wo), f32),
+            pltpu.VMEM((seq_count, 1, 128), i32),
+            pltpu.VMEM((total, wo), f32),
+            pltpu.VMEM((layers, share, wo), f32),
+            pltpu.VMEM((layers, total, wo), i16),
+            pltpu.VMEM((layers, vocab_count, share, wo), i16),
             pltpu.VMEM((layers, total, wo), bf16),
             pltpu.VMEM((layers, vocab_count, 1, total), f32),
             pltpu.VMEM((layers, 1, total), f32),
@@ -606,7 +715,7 @@
             dma((layers - 1,)),
             dma((seq_count,)),
             dma((seq_count,)),
-            dma((layers, chips)),
+            dma((layers, chips, 2)),
             dma((layers, chips)),
             dma((layers, chips)),
             dma((layers, chips)),
@@ -631,7 +740,7 @@
             collective_id=0, has_side_effects=True, vmem_limit_bytes=63 << 20
         ),
         name="readout",
-    )(probed, final, meta, bias, gain, translator, unembed)
+    )(rows, count, wanted, bias, gain, translator, unembed)
 
 
 def body(
@@ -647,38 +756,20 @@
 ):
     seq_count = lax.axis_size("seq")
     vocab_count = lax.axis_size("vocab")
-    seq_index = lax.axis_index("seq")
-    layers = probe_states.shape[0]
-    cap = answer_rows.shape[1]
     model = probe_states.shape[2] * vocab_count
-    picks = answer_rows[0]
-
-    probed = jnp.take(probe_states, picks, axis=1, mode="clip")
-    final = jnp.take(final_states, picks, axis=0, mode="clip")
-    lane = jnp.arange(seq_count * cap, dtype=i32)[None, :]
-    line = jnp.arange(8, dtype=i32)[:, None]
-    mine = lane // cap == seq_index
-    after = lane // cap > seq_index
-    meta = jnp.where(jnp.logical_and(line == 0, mine), answer_count[0], 0)
-    meta = jnp.where(jnp.logical_and(line == 1, mine), jnp.tile(targets, (1, seq_count)), meta)
-    meta = jnp.where(jnp.logical_and(line == 2, after), answer_count[0], meta)
-
-    out = readout(
-        probed,
-        final,
-        meta,
-        translator_bias[:, None, :],
-        norm_gain[None, :],
+    return readout(
+        pick(answer_rows, probe_states, final_states),
+        answer_count,
+        targets,
+        translator_bias,
+        norm_gain,
         translator,
         unembed,
         seq_count,
         vocab_count,
-        cap,
         seq_count * FLAG_DEV,
         model,
     )
-    flat = out[:, : 2 * layers + 1].T
-    return (flat[: layers + 1, None, :], flat[layers + 1 :, None, :])
 
 
 def solution(mesh):

time: 128 us -> 109 us (0.85)
  local copies, waits for them, and re-layouts: 11.8 us -> 2.48 us
  Pallas kernels: 113 us -> 105 us
  other arithmetic: 1.35 us -> 0 us
    pallas_call x1 -> x2, Pallas kernels: 113 us -> 105 us  [the longest x1 101 us: readout(): pl.pallas_call(body, out_shape=(jax.ShapeDtypeStruct((layers, 1, cap), f3...]
    gather x2 -> x0, local copies, waits for them, and re-layouts: 6.41 us -> none  [the longest x1 3.65 us: body(): final = jnp.take(final_states, picks, axis=0, mode='clip')]
    broadcast_in_dim x4 -> x0, local copies, waits for them, and re-layouts: 2.67 us -> none  [the longest x1 1.31 us: body(): translator_bias[:, None, :]]
where the time goes in v2:
time: 109 us
  Pallas kernels  105 us (96%)
  local copies, waits for them, and re-layouts  2.48 us (2%)
  between operations  1.29 us (1%)
    pallas_call x1, Pallas kernels, readout(): pl.pallas_call(body, out_shape=(jax.ShapeDtypeStruct((layers, 1, cap), f3...  101 us
    pallas_call x1, Pallas kernels, pick(): pl.pallas_call(lambda *refs: pick_kernel(layers, cap, *refs), out_shape=j...  4.3 us
    unnamed x2, local copies, waits for them, and re-layouts  2.48 us

profile of v2, /device:TPU:0, one launch (start us, length us, event | category | flops | bytes accessed | tf_op | source)
XLA Modules:
  0.0 109.2 jit_solution(9755209154009714729)
XLA Ops:
  1.3 4.3 %pick.1.refs_0_ = bf16[4,32,1536]{2,1,0:T(8,128)(2,1)} custom-call(s32[1,32]{1,0:T(1,128)} %refs_0_.1, bf16[3,1024,1536]{2,1,0:T(8,128)(2,1)} %refs_1_.2, bf16[1024,1536]{1,0:T(8,128)(2,1)} %refs_2_.2), custom_call_target="tpu_custom_call" | custom-call | tf_op jit(solution)/shard_map/pick/pallas_call | solution.py:651
  5.6 101.1 %readout.1 = (f32[4,1,32]{2,1,0:T(1,128)}, f32[3,1,32]{2,1,0:T(1,128)}) custom-call(bf16[4,32,1536]{2,1,0:T(8,128)(2,1)} %pick.1.refs_0_, s32[1]{0:T(128)S(6)} %copy.13.refs_1_, s32[1,32]{1,0:T(1,128)} %refs_2_.3, f32[3,768]{1,0:T(4,128)} %refs_3_.1, f32[768]{0:T(1024)} %refs_4_.1, bf16[3,1536,768]{2,1,0:T(8,128)(2,1)} %refs_5_.1, bf16[8192,768]{1,0:T(8,128)(2,1)} %refs_6_.1), custom_call_target="tpu_custom_call" | custom-call | tf_op jit(solution)/shard_map/readout/pallas_call | solution.py:675
  106.7 1.2 %copy.14 = f32[4,1,32]{2,1,0:T(1,128)} copy(f32[4,1,32]{2,1,0:T(1,128)} %get-tuple-element.4) | data formatting | bytes 1024
  107.9 1.2 %copy.15 = f32[3,1,32]{2,1,0:T(1,128)} copy(f32[3,1,32]{2,1,0:T(1,128)} %get-tuple-element.5) | data formatting | bytes 768

commit v3 on v2

--- a/solution.py
+++ b/solution.py
@@ -16,7 +16,6 @@
 MESH = pl.DeviceIdType.MESH
 f32, bf16, i16, i32 = jnp.float32, jnp.bfloat16, jnp.int16, jnp.int32
 
-
 class Code:
     def __init__(self, widest):
         self.knee = 7.5e-4
@@ -30,7 +29,6 @@
         level = code.astype(i32).astype(f32)
         size = (jnp.exp2(jnp.abs(level) * (1.0 / self.scale)) - 1.0) * self.knee
         return jnp.where(level < 0, -size, size)
-
 
 def kernel(
     layers, total, cap, seq_count, vocab_count, model, code, xcode,
@@ -44,11 +42,11 @@
     seq, voc = lax.axis_index("seq"), lax.axis_index("vocab")
     chip, core = seq // 2, seq % 2
     chips = seq_count // 2
-    vp, wo = u.shape
+    chunk, wo = u.shape[3], u.shape[4]
+    vp = 4 * CHUNKS * chunk
     wi = picked_rows.shape[2]
     ratio = wi // wo
     half, quarter = vp // 2, vp // 4
-    chunk = quarter // CHUNKS
     steps = layers * CHUNKS
     plane = 2 * vocab_count
     share = total // vocab_count
@@ -59,12 +57,8 @@
     home = (voc * ratio) // 2
     at_home = chip == home
 
-    pieces = 4 * CHUNKS
-    piece = vp // pieces
-
     def u_copy(k):
-        part = pl.ds(pl.multiple_of(k * piece, piece), piece)
-        return pltpu.make_async_copy(u_hbm.at[part], u.at[part], u_sem.at[k])
+        return pltpu.make_async_copy(u_hbm.at[:, :, k], u.at[:, :, k], u_sem.at[k])
 
     def t_copy(l):
         return pltpu.make_async_copy(t_hbm.at[l], tr.at[l], t_sem.at[l])
@@ -77,11 +71,16 @@
     meta[...] = jnp.full(meta.shape, count[0], i32)
     meta[:, :cap] = wanted_ref[...]
 
+    def settle(what, sem):
+        return remote(what, what, sem, sem, partner)
+
+    partner = (chip * 2 + 1 - core, voc)
+
     @pl.loop(0, layers - 1)
     def _(l):
         t_copy(l).start()
 
-    @pl.loop(0, pieces)
+    @pl.loop(0, CHUNKS)
     def _(k):
         u_copy(k).start()
 
@@ -103,8 +102,6 @@
         q = lax.rem(voc + p, vocab_count)
         return q, (seq, q)
 
-    partner = (chip * 2 + 1 - core, voc)
-
     @pl.loop(1, plane)
     def _(p):
         pl.semaphore_signal(barrier, inc=1, device_id=in_plane(p)[1], device_id_type=MESH)
@@ -117,7 +114,7 @@
         pl.semaphore_wait(barrier, plane - 1 + seq_count - 1)
 
     def meta_copy(p, slot):
-        return remote(meta, meta_recv.at[slot], msend_sem.at[p], mrecv_sem.at[slot], in_column(p)[1])
+        return remote(meta, meta_recv.at[slot], msend_sem.at[0], mrecv_sem.at[0], in_column(p)[1])
 
     @pl.loop(1, seq_count)
     def _(p):
@@ -135,7 +132,7 @@
         to = jnp.minimum(chip + 1, chips - 1) if d == 0 else jnp.maximum(chip - 1, 0)
         here = rows.at[i, block(source * 2 + core)]
         return remote(
-            here if src is None else src, here, rsend_sem.at[i, source, d], rrecv_sem.at[i, source], (to * 2 + core, voc)
+            here if src is None else src, here, rsend_sem.at[i, d], rrecv_sem.at[i, source], (to * 2 + core, voc)
         )
 
     def passes(d):
@@ -143,11 +140,11 @@
 
     def home_copy(source):
         here = rows.at[0, block(source * 2 + core)]
-        return remote(picked_rows.at[0], here, rsend_sem.at[0, chip, 0], rrecv_sem.at[0, source], (home * 2 + core, voc))
-
-    def forward_copy(i, source, other, src=None):
-        part = rows.at[i, block(source * 2 + (1 - core if other else core))]
-        return remote(part if src is None else src, part, fsend_sem.at[i, source], frecv_sem.at[i, source], partner)
+        return remote(picked_rows.at[0], here, rsend_sem.at[0, 0], rrecv_sem.at[0, source], (home * 2 + core, voc))
+
+    def forward_copy(i, source, src=None):
+        part = rows.at[i, block(source * 2 + core)]
+        return remote(part if src is None else src, part, fsend_sem.at[i], frecv_sem.at[i], partner)
 
     def depart(i):
         for d in range(2):
@@ -155,11 +152,11 @@
             def _():
                 row_copy(i, chip, d, row_src(i)).start()
 
-        forward_copy(i, chip, False, row_src(i)).start()
+        forward_copy(i, chip, row_src(i)).start()
 
     @pl.when(at_home)
     def _():
-        forward_copy(0, chip, False, picked_rows.at[0]).start()
+        forward_copy(0, chip, picked_rows.at[0]).start()
 
     @pl.when(jnp.logical_not(at_home))
     def _():
@@ -176,11 +173,7 @@
     acc[...] = jnp.zeros_like(acc)
 
     def places():
-        @pl.loop(1, seq_count)
-        def _(p):
-            q, _ = in_column(p)
-            meta_copy(p, q).wait_recv()
-
+        settle(meta_recv.at[pl.ds(0, seq_count - 1)], mrecv_sem.at[0]).wait_recv()
         every = jnp.concatenate([meta_recv[q] for q in range(seq_count)], axis=0)
         slots = seq_count * cap
         lane = lax.broadcasted_iota(i32, (1, slots), 1)
@@ -223,7 +216,7 @@
         def _(p):
             q, _ = in_line(p)
             home_copy(q).wait_recv()
-            forward_copy(0, q, False).start()
+            forward_copy(0, q).start()
 
     def relay(i):
         @pl.loop(1, chips)
@@ -239,7 +232,7 @@
                     def _():
                         row_copy(i, source, d).start()
 
-                    forward_copy(i, source, False).start()
+                    forward_copy(i, source).start()
 
     def early(i):
         pl.when(jnp.logical_and(i == 0, at_home))(gather_home)
@@ -262,14 +255,12 @@
     def group_copy(i, p, slot):
         q, there = in_group(p)
         return remote(
-            rs_src.at[i, part_of(q)], rs_recv.at[i, slot], gsend_sem.at[i, p], grecv_sem.at[i, slot], there
+            rs_src.at[i, part_of(q)], rs_recv.at[i, slot], gsend_sem.at[i], grecv_sem.at[i], there
         )
 
     def translate(i):
         def go():
-            @pl.loop(0, chips)
-            def _(q):
-                forward_copy(i, q, True).wait_recv()
+            settle(rows.at[i, pl.ds(0, chips * cap)], frecv_sem.at[i]).wait_recv()
 
             packed[...] = jnp.dot(hit[...], rows[i], preferred_element_type=f32).astype(bf16)
 
@@ -305,13 +296,13 @@
 
     def y_copy(i, p, owner):
         return remote(
-            y.at[i, part_of(owner)], y.at[i, part_of(owner)], ysend_sem.at[i, p], yrecv_sem.at[i, owner],
+            y.at[i, part_of(owner)], y.at[i, part_of(owner)], ysend_sem.at[i], yrecv_sem.at[i],
             in_group(p)[1],
         )
 
     def sq_copy(i, p, owner):
         return remote(
-            sq_part.at[i, owner], sq_part.at[i, owner], qsend_sem.at[i, p], qrecv_sem.at[i, owner], in_group(p)[1]
+            sq_part.at[i, owner], sq_part.at[i, owner], qsend_sem.at[i], qrecv_sem.at[i], in_group(p)[1]
         )
 
     def scale(i):
@@ -332,10 +323,10 @@
 
         @pl.when(i > 0)
         def _():
+            settle(rs_recv.at[i, pl.ds(0, vocab_count - 1)], grecv_sem.at[i]).wait_recv()
             x = rs_own[i] + bias[pl.ds(i - 1, 1), :]
             for p in range(1, vocab_count):
                 q, _ = in_group(p)
-                group_copy(i, p, q).wait_recv()
                 x = x + xcode.dec(rs_recv[i, q])
             go(x)
 
@@ -345,7 +336,7 @@
 
         @pl.when(jnp.logical_and(i == 0, jnp.logical_not(holds)))
         def _():
-            group_copy(0, 1, holder).wait_recv()
+            settle(rs_recv.at[0, 0], grecv_sem.at[0]).wait_recv()
             go(xcode.dec(rs_recv[0, holder]))
 
     def end_device(e):
@@ -353,15 +344,12 @@
 
     def v_copy(i, e, source):
         return remote(
-            sq_src.at[i], sq_recv.at[i, source], vsend_sem.at[i, e], vrecv_sem.at[i, source], (end_device(e), voc)
+            sq_src.at[i], sq_recv.at[i, source], vsend_sem.at[i], vrecv_sem.at[i], (end_device(e), voc)
         )
 
     def collect(i):
-        @pl.loop(1, vocab_count)
-        def _(p):
-            q, _ = in_group(p)
-            y_copy(i, p, q).wait_recv()
-            sq_copy(i, p, q).wait_recv()
+        settle(y.at[i, pl.ds(0, (vocab_count - 1) * share)], yrecv_sem.at[i]).wait_recv()
+        settle(sq_part.at[i, pl.ds(0, vocab_count - 1)], qrecv_sem.at[i]).wait_recv()
 
         sums = sq_part[i, 0]
         for q in range(1, vocab_count):
@@ -386,15 +374,11 @@
     def line_copy(k, d):
         to = jnp.minimum(chip + 1, chips - 1) if d == 0 else jnp.maximum(chip - 1, 0)
         return remote(
-            zsend.at[k, d], zrecv.at[k, d], zsend_sem.at[k, d], zrecv_sem.at[k, d], (to * 2 + core, voc)
-        )
-
-    def rows_at(owner, d, j):
-        start = owner * half + d * quarter + j * chunk
-        return pl.ds(pl.multiple_of(start, chunk), chunk)
-
-    def product(part, yl):
-        return lax.dot_general(u[part, :], yl, (((1,), (1,)), ((), ())), preferred_element_type=f32)
+            zsend.at[d, k], zrecv.at[k, d], zsend_sem.at[d], zrecv_sem.at[k, d], (to * 2 + core, voc)
+        )
+
+    def product(owner, d, j, yl):
+        return lax.dot_general(u[owner, d, j], yl, (((1,), (1,)), ((), ())), preferred_element_type=f32)
 
     def fold(value):
         return jnp.sum(value.reshape(chunk // 8, 8, total), axis=0)
@@ -404,10 +388,7 @@
 
         @pl.when(j == 0)
         def _():
-            @pl.loop(1, seq_count)
-            def _(p):
-                q, _ = in_column(p)
-                v_copy(i, 0, q).wait_recv()
+            settle(sq_recv.at[i, pl.ds(0, seq_count - 1)], vrecv_sem.at[i]).wait_recv()
 
             squares = sq_recv[i, 0]
             for q in range(1, seq_count):
@@ -442,7 +423,7 @@
 
         @pl.when(jnp.logical_not(last))
         def _():
-            zsend[k, d] = code.enc(own[k, d])
+            zsend[d, k] = code.enc(own[k, d])
             line_copy(k, d).start()
 
         @pl.when(last)
@@ -471,8 +452,7 @@
 
         @pl.when(jnp.logical_and(t >= 0, t < CHUNKS))
         def _():
-            for part in range(4):
-                u_copy(part * CHUNKS + t).wait()
+            u_copy(t).wait()
 
         @pl.when(jnp.logical_and(t >= 0, t < steps))
         def _():
@@ -485,10 +465,10 @@
                 pair_copy(t - SLOTS).wait_send()
 
             for d in range(2):
-                psend[lax.rem(t, SLOTS), d] = product(rows_at(1 - core, d, j), yl)
+                psend[lax.rem(t, SLOTS), d] = product(1 - core, d, j, yl)
             pair_copy(t).start()
             for d in range(2):
-                own[t, d] = product(rows_at(core, d, j), yl)
+                own[t, d] = product(core, d, j, yl)
             scope.__exit__(None, None, None)
 
         @pl.when(jnp.logical_and(t >= 1, t <= steps))
@@ -506,12 +486,12 @@
                     forward(k, d)
 
     def stat_copy(p, slot):
-        return remote(stat_send, stat_recv.at[slot], ssend_sem.at[p], srecv_sem.at[slot], in_plane(p)[1])
+        return remote(stat_send, stat_recv.at[slot], ssend_sem.at[0], srecv_sem.at[0], in_plane(p)[1])
 
     end = jnp.where(chip == 0, 0, 1)
 
     def line_stat(p, side):
-        return remote(line_send, line_recv.at[side], lsend_sem.at[p], lrecv_sem.at[side], in_line(p)[1])
+        return remote(line_send, line_recv.at[side], lsend_sem.at[0], lrecv_sem.at[side], in_line(p)[1])
 
     @pl.when(at_end)
     def _():
@@ -528,9 +508,7 @@
             stat_copy(p, me).start()
 
         with jax.named_scope('planewait'):
-            @pl.loop(1, plane)
-            def _(p):
-                stat_copy(p, in_plane(p)[0]).wait_recv()
+            settle(stat_recv.at[pl.ds(0, plane - 1)], srecv_sem.at[0]).wait_recv()
 
         full = stat_recv[0]
         for q in range(1, plane):
@@ -542,60 +520,50 @@
         def _(p):
             line_stat(p, end).start()
 
-    @pl.loop(1, seq_count)
-    def _(p):
-        meta_copy(p, seq).wait_send()
+    settle(meta_recv.at[pl.ds(0, seq_count - 1)], msend_sem.at[0]).wait_send()
 
     @pl.loop(0, layers)
     def _(i):
-        @pl.loop(0, chips)
-        def _(q):
+        for c in range(chips):
             for d in range(2):
-                @pl.when(jnp.logical_and(jnp.logical_and(i > 0, passes(d)), q <= chip if d == 0 else q >= chip))
-                def _():
-                    row_copy(i, q, d).wait_send()
+                count_d = c + 1 if d == 0 else chips - c
+                if (c < chips - 1) if d == 0 else (c > 0):
+                    @pl.when(jnp.logical_and(i > 0, chip == c))
+                    def _():
+                        settle(rows.at[i, pl.ds(0, count_d * cap)], rsend_sem.at[i, d]).wait_send()
 
         @pl.when(jnp.logical_or(i > 0, at_home))
         def _():
-            @pl.loop(0, chips)
-            def _(q):
-                forward_copy(i, q, False).wait_send()
-
-        @pl.loop(1, vocab_count)
-        def _(p):
-            @pl.when(jnp.logical_or(i > 0, holds))
-            def _():
-                group_copy(i, p, voc).wait_send()
-
-            y_copy(i, p, voc).wait_send()
-            sq_copy(i, p, voc).wait_send()
-
-        @pl.loop(0, 4)
-        def _(e):
-            @pl.when(end_device(e) != seq)
-            def _():
-                v_copy(i, e, seq).wait_send()
+            settle(rows.at[i, pl.ds(0, chips * cap)], fsend_sem.at[i]).wait_send()
+
+        @pl.when(jnp.logical_or(i > 0, holds))
+        def _():
+            settle(rs_recv.at[i, pl.ds(0, vocab_count - 1)], gsend_sem.at[i]).wait_send()
+
+        settle(y.at[i, pl.ds(0, (vocab_count - 1) * share)], ysend_sem.at[i]).wait_send()
+        settle(sq_part.at[i, pl.ds(0, vocab_count - 1)], qsend_sem.at[i]).wait_send()
+
+        @pl.when(at_end)
+        def _():
+            settle(sq_recv.at[i, pl.ds(0, 3)], vsend_sem.at[i]).wait_send()
+
+        @pl.when(jnp.logical_not(at_end))
+        def _():
+            settle(sq_recv.at[i, pl.ds(0, 4)], vsend_sem.at[i]).wait_send()
 
     @pl.loop(steps - SLOTS, steps)
     def _(t):
         pair_copy(t).wait_send()
 
-    @pl.loop(0, steps)
-    def _(k):
-        for d in range(2):
-            @pl.when(chip != (chips - 1 if d == 0 else 0))
-            def _():
-                line_copy(k, d).wait_send()
+    for d in range(2):
+        @pl.when(chip != (chips - 1 if d == 0 else 0))
+        def _():
+            settle(zsend.at[d], zsend_sem.at[d]).wait_send()
 
     @pl.when(at_end)
     def _():
-        @pl.loop(1, plane)
-        def _(p):
-            stat_copy(p, me).wait_send()
-
-        @pl.loop(1, chips)
-        def _(p):
-            line_stat(p, end).wait_send()
+        settle(stat_recv.at[pl.ds(0, plane - 1)], ssend_sem.at[0]).wait_send()
+        settle(stat_recv.at[pl.ds(0, chips - 1)], lsend_sem.at[0]).wait_send()
 
     for side in range(2):
         @pl.when(chip != (0 if side == 0 else chips - 1))
@@ -625,7 +593,6 @@
         kl_ref[l] = turned[layers + l : layers + l + 1]
     scope2.__exit__(None, None, None)
 
-
 def pick_kernel(layers, cap, picks, probe_hbm, final_hbm, out_ref, found, sem):
     @pl.loop(0, cap)
     def _(k):
@@ -643,7 +610,6 @@
     for l in range(layers):
         pltpu.make_async_copy(found.at[l], found.at[l], sem.at[l]).wait()
         out_ref[l] = jnp.dot(match, found[l], preferred_element_type=f32).astype(bf16)
-
 
 def pick(answer_rows, probe_states, final_states):
     layers, cap, wi = probe_states.shape[0] + 1, answer_rows.shape[1], final_states.shape[1]
@@ -656,7 +622,6 @@
         scratch_shapes=[pltpu.VMEM((layers, cap * PACK, wi), bf16), pltpu.SemaphoreType.DMA((layers,))],
         name="pick",
     )(answer_rows, probe_states, final_states)
-
 
 def readout(rows, count, wanted, bias, gain, translator, unembed, seq_count, vocab_count, total, model):
     layers, cap, wi = rows.shape
@@ -681,7 +646,7 @@
         in_specs=[vmem, pl.BlockSpec(memory_space=pltpu.SMEM), vmem, vmem, vmem, hbm, hbm],
         out_specs=(vmem, vmem),
         scratch_shapes=[
-            pltpu.VMEM((vp, wo), bf16),
+            pltpu.VMEM((2, 2, CHUNKS, chunk, wo), bf16),
             pltpu.VMEM((layers - 1, wi, wo), bf16),
             pltpu.VMEM((1, 128), i32),
             pltpu.VMEM((layers, seq_count * cap, wi), bf16),
@@ -702,7 +667,7 @@
             pltpu.VMEM((steps, 2, chunk, total), f32),
             pltpu.VMEM((SLOTS, 2, chunk, total), f32),
             pltpu.VMEM((steps, 2, chunk, total), f32),
-            pltpu.VMEM((steps, 2, chunk, total), i16),
+            pltpu.VMEM((2, steps, chunk, total), i16),
             pltpu.VMEM((steps, 2, chunk, total), i16),
             pltpu.VMEM((CHUNKS, chunk, total), f32),
             pltpu.VMEM((CHUNKS, chunk, total), f32),
@@ -711,37 +676,36 @@
             pltpu.VMEM((plane, deep, total), f32),
             pltpu.VMEM((deep, total), f32),
             pltpu.VMEM((2, deep, total), f32),
-            dma((4 * CHUNKS,)),
+            dma((CHUNKS,)),
             dma((layers - 1,)),
-            dma((seq_count,)),
-            dma((seq_count,)),
-            dma((layers, chips, 2)),
+            dma((1,)),
+            dma((1,)),
+            dma((layers, 2)),
             dma((layers, chips)),
-            dma((layers, chips)),
-            dma((layers, chips)),
-            dma((layers, vocab_count)),
-            dma((layers, vocab_count)),
-            dma((layers, vocab_count)),
-            dma((layers, vocab_count)),
-            dma((layers, vocab_count)),
-            dma((layers, vocab_count)),
-            dma((layers, 4)),
-            dma((layers, seq_count)),
+            dma((layers,)),
+            dma((layers,)),
+            dma((layers,)),
+            dma((layers,)),
+            dma((layers,)),
+            dma((layers,)),
+            dma((layers,)),
+            dma((layers,)),
+            dma((layers,)),
+            dma((layers,)),
             dma((SLOTS,)),
             dma((steps,)),
+            dma((2,)),
             dma((steps, 2)),
-            dma((steps, 2)),
-            dma((plane,)),
-            dma((plane,)),
-            dma((chips,)),
+            dma((1,)),
+            dma((1,)),
+            dma((1,)),
             dma((2,)),
         ],
         compiler_params=pltpu.CompilerParams(
             collective_id=0, has_side_effects=True, vmem_limit_bytes=63 << 20
         ),
         name="readout",
-    )(rows, count, wanted, bias, gain, translator, unembed)
-
+    )(rows, count, wanted, bias, gain, translator, unembed.reshape(2, 2, CHUNKS, chunk, wo))
 
 def body(
     probe_states,
@@ -771,7 +735,6 @@
         model,
     )
 
-
 def solution(mesh):
     in_specs = (
         P(None, "seq", "vocab"),

time: 109 us -> 107 us (0.982)
  Pallas kernels: 105 us -> 103 us
    pallas_call x1, Pallas kernels: 101 us -> 98.8 us  [readout(): pl.pallas_call(body, out_shape=(jax.ShapeDtypeStruct((layers, 1, cap), f3...]
where the time goes in v3:
time: 107 us
  Pallas kernels  103 us (96%)
  local copies, waits for them, and re-layouts  2.48 us (2%)
  between operations  1.29 us (1%)
    pallas_call x1, Pallas kernels, readout(): pl.pallas_call(body, out_shape=(jax.ShapeDtypeStruct((layers, 1, cap), f3...  98.8 us
    pallas_call x1, Pallas kernels, pick(): pl.pallas_call(lambda *refs: pick_kernel(layers, cap, *refs), out_shape=j...  4.3 us
    unnamed x2, local copies, waits for them, and re-layouts  2.48 us

profile of v3, /device:TPU:0, one launch (start us, length us, event | category | flops | bytes accessed | tf_op | source)
XLA Modules:
  0.0 106.9 jit_solution(12819304215003332156)
XLA Ops:
  1.3 4.3 %pick.1.refs_0_ = bf16[4,32,1536]{2,1,0:T(8,128)(2,1)} custom-call(s32[1,32]{1,0:T(1,128)} %refs_0_.1, bf16[3,1024,1536]{2,1,0:T(8,128)(2,1)} %refs_1_.2, bf16[1024,1536]{1,0:T(8,128)(2,1)} %refs_2_.2), custom_call_target="tpu_custom_call" | custom-call | tf_op jit(solution)/shard_map/pick/pallas_call | solution.py:617
  5.6 98.8 %readout.1 = (f32[4,1,32]{2,1,0:T(1,128)}, f32[3,1,32]{2,1,0:T(1,128)}) custom-call(bf16[4,32,1536]{2,1,0:T(8,128)(2,1)} %pick.1.refs_0_, s32[1]{0:T(128)S(6)} %copy.13.refs_1_, s32[1,32]{1,0:T(1,128)} %refs_2_.3, f32[3,768]{1,0:T(4,128)} %refs_3_.1, f32[768]{0:T(1024)} %refs_4_.1, bf16[3,1536,768]{2,1,0:T(8,128)(2,1)} %refs_5_.1, ...), custom_call_target="tpu_custom_call" | custom-call | tf_op jit(solution)/shard_map/readout/pallas_call | solution.py:640
  104.4 1.2 %copy.14 = f32[4,1,32]{2,1,0:T(1,128)} copy(f32[4,1,32]{2,1,0:T(1,128)} %get-tuple-element.4) | data formatting | bytes 1024
  105.6 1.2 %copy.15 = f32[3,1,32]{2,1,0:T(1,128)} copy(f32[3,1,32]{2,1,0:T(1,128)} %get-tuple-element.5) | data formatting | bytes 768

commit v4 on v3

--- a/solution.py
+++ b/solution.py
@@ -32,7 +32,7 @@
 
 def kernel(
     layers, total, cap, seq_count, vocab_count, model, code, xcode,
-    picked_rows, count, wanted_ref, bias, gain, t_hbm, u_hbm, prob_ref, kl_ref,
+    picked_rows, count, wanted_ref, bias, gain, t_hbm, u_hbm, out_ref,
     u, tr, meta, rows, packed, hit, tgt, spot_col, meta_recv, part, rs_own, rs_src, rs_recv, y, sq_part, sq_src, sq_recv, fac,
     own, psend, precv, zsend, zrecv, z3, e3, acc, stat_send, stat_recv, line_send, line_recv,
     u_sem, t_sem, msend_sem, mrecv_sem, rsend_sem, rrecv_sem, fsend_sem, frecv_sem, gsend_sem, grecv_sem,
@@ -68,6 +68,32 @@
             src_ref=src, dst_ref=dst, send_sem=send, recv_sem=recv, device_id=device, device_id_type=MESH
         )
 
+    barrier = pltpu.get_barrier_semaphore()
+
+    def in_plane(p):
+        q = lax.rem(me + p, plane)
+        return q, (chip * 2 + q // vocab_count, lax.rem(q, vocab_count))
+
+    def in_line(p):
+        q = lax.rem(chip + p, chips)
+        return q, (q * 2 + core, voc)
+
+    def in_column(p):
+        q = lax.rem(seq + p, seq_count)
+        return q, (q, voc)
+
+    def in_group(p):
+        q = lax.rem(voc + p, vocab_count)
+        return q, (seq, q)
+
+    @pl.loop(1, plane)
+    def _(p):
+        pl.semaphore_signal(barrier, inc=1, device_id=in_plane(p)[1], device_id_type=MESH)
+
+    @pl.loop(1, seq_count)
+    def _(p):
+        pl.semaphore_signal(barrier, inc=1, device_id=in_column(p)[1], device_id_type=MESH)
+
     meta[...] = jnp.full(meta.shape, count[0], i32)
     meta[:, :cap] = wanted_ref[...]
 
@@ -83,32 +109,6 @@
     @pl.loop(0, CHUNKS)
     def _(k):
         u_copy(k).start()
-
-    barrier = pltpu.get_barrier_semaphore()
-
-    def in_plane(p):
-        q = lax.rem(me + p, plane)
-        return q, (chip * 2 + q // vocab_count, lax.rem(q, vocab_count))
-
-    def in_line(p):
-        q = lax.rem(chip + p, chips)
-        return q, (q * 2 + core, voc)
-
-    def in_column(p):
-        q = lax.rem(seq + p, seq_count)
-        return q, (q, voc)
-
-    def in_group(p):
-        q = lax.rem(voc + p, vocab_count)
-        return q, (seq, q)
-
-    @pl.loop(1, plane)
-    def _(p):
-        pl.semaphore_signal(barrier, inc=1, device_id=in_plane(p)[1], device_id_type=MESH)
-
-    @pl.loop(1, seq_count)
-    def _(p):
-        pl.semaphore_signal(barrier, inc=1, device_id=in_column(p)[1], device_id_type=MESH)
 
     with jax.named_scope('barrier'):
         pl.semaphore_wait(barrier, plane - 1 + seq_count - 1)
@@ -586,11 +586,7 @@
     for l, value in enumerate(result):
         column = jnp.sum(jnp.where(owned, value, 0.0), axis=1, keepdims=True)
         out = jnp.where(place == l, column, out)
-    turned = out.T
-    for l in range(layers):
-        prob_ref[l] = turned[l : l + 1]
-    for l in range(layers - 1):
-        kl_ref[l] = turned[layers + l : layers + l + 1]
+    out_ref[...] = out
     scope2.__exit__(None, None, None)
 
 def pick_kernel(layers, cap, picks, probe_hbm, final_hbm, out_ref, found, sem):
@@ -639,12 +635,9 @@
     body = lambda *refs: kernel(layers, total, cap, seq_count, vocab_count, model, code, xcode, *refs)
     return pl.pallas_call(
         body,
-        out_shape=(
-            jax.ShapeDtypeStruct((layers, 1, cap), f32),
-            jax.ShapeDtypeStruct((layers - 1, 1, cap), f32),
-        ),
+        out_shape=jax.ShapeDtypeStruct((cap, 128), f32),
         in_specs=[vmem, pl.BlockSpec(memory_space=pltpu.SMEM), vmem, vmem, vmem, hbm, hbm],
-        out_specs=(vmem, vmem),
+        out_specs=vmem,
         scratch_shapes=[
             pltpu.VMEM((2, 2, CHUNKS, chunk, wo), bf16),
             pltpu.VMEM((layers - 1, wi, wo), bf16),
@@ -721,7 +714,8 @@
     seq_count = lax.axis_size("seq")
     vocab_count = lax.axis_size("vocab")
     model = probe_states.shape[2] * vocab_count
-    return readout(
+    layers = probe_states.shape[0]
+    out = readout(
         pick(answer_rows, probe_states, final_states),
         answer_count,
         targets,
@@ -734,6 +728,8 @@
         seq_count * FLAG_DEV,
         model,
     )
+    flat = out[:, : 2 * layers + 1].T
+    return flat[: layers + 1, None, :], flat[layers + 1 :, None, :]
 
 def solution(mesh):
     in_specs = (

time: 107 us -> 107 us (level)
    unnamed x2, local copies, waits for them, and re-layouts: 2.48 us -> 1.29 us
where the time goes in v4:
time: 107 us; the launch traced here: 106 us
  Pallas kernels  103 us (96%)
  local copies, waits for them, and re-layouts  2.09 us (2%)
  between operations  1.3 us (1%)
    pallas_call x1, Pallas kernels, readout(): pl.pallas_call(body, out_shape=jax.ShapeDtypeStruct((cap, 128), f32), in_...  98.6 us
    pallas_call x1, Pallas kernels, pick(): pl.pallas_call(lambda *refs: pick_kernel(layers, cap, *refs), out_shape=j...  4.3 us

profile of v4, /device:TPU:0, one launch (start us, length us, event | category | flops | bytes accessed | tf_op | source)
XLA Modules:
  0.0 106.3 jit_solution(4046797608486714533)
XLA Ops:
  1.3 4.3 %pick.1.refs_0_ = bf16[4,32,1536]{2,1,0:T(8,128)(2,1)} custom-call(s32[1,32]{1,0:T(1,128)} %refs_0_.1, bf16[3,1024,1536]{2,1,0:T(8,128)(2,1)} %refs_1_.2, bf16[1024,1536]{1,0:T(8,128)(2,1)} %refs_2_.2), custom_call_target="tpu_custom_call" | custom-call | tf_op jit(solution)/shard_map/pick/pallas_call | solution.py:613
  5.6 98.6 %readout.1 = f32[32,128]{1,0:T(8,128)} custom-call(bf16[4,32,1536]{2,1,0:T(8,128)(2,1)} %pick.1.refs_0_, s32[1]{0:T(128)S(6)} %copy.19.refs_1_, s32[1,32]{1,0:T(1,128)} %refs_2_.3, f32[3,768]{1,0:T(4,128)} %refs_3_.1, f32[768]{0:T(1024)} %refs_4_.1, bf16[3,1536,768]{2,1,0:T(8,128)(2,1)} %refs_5_.1, bf16[2,2,4,512,768]{4,3,2,1,0:T(8,128)(2,1)} %bitcast.7), custom_call_target="tpu_custom_call" | custom-call | tf_op jit(solution)/shard_map/readout/pallas_call | solution.py:636
  104.2 0.7 slice_bitcast_fusion.2
  104.9 0.1 slice_bitcast_fusion
  105.0 0.6 copy.14
  105.7 0.7 copy.13
  (1 shorter events, 0.0 us)
